TPU v7x, 32 devices: a whole 2x2x4 slice. The times are simulated.
32 devices in a mesh: gp: 32 (over z, y, x, core).
Axes of the slice: x: 2, y: 2, z: 4, core: 2. Of those that a mesh axis runs over, the one named last changes fastest.
Arguments:
- grid_in: bfloat16 [16384, 474], P('gp')
- mesh_static: bfloat16 [16384, 3], P('gp')
- edge_static: bfloat16 [24576, 4], P('gp')
- send_rows: int32 [1024, 16], P('gp')
- edge_src: int32 [24576], P('gp')
- edge_dst: int32 [24576], P('gp')
- w_grid_in: bfloat16 [474, 512], replicated
- w_mesh_in: bfloat16 [3, 512], replicated
- w_edge_in: bfloat16 [4, 512], replicated
- w_edge_up: bfloat16 [1536, 512], replicated
- w_mesh_up: bfloat16 [1024, 512], replicated
- w_grid_up: bfloat16 [512, 512], replicated
- w_second: bfloat16 [6, 512, 512], replicated
- vectors: float32 [6, 4, 512], replicated
- d_mesh_out: bfloat16 [16384, 512], P('gp')
- d_grid_out: bfloat16 [16384, 512], P('gp')
Outputs:
- output 1: bfloat16 [16384, 512], P('gp')
- output 2: bfloat16 [16384, 512], P('gp')
- output 3: float32 [16384, 474], P('gp')
- output 4: float32 [474, 512], replicated
- output 5: float32 [3, 512], replicated
- output 6: float32 [4, 512], replicated
- output 7: float32 [1536, 512], replicated
- output 8: float32 [1024, 512], replicated
- output 9: float32 [512, 512], replicated
- output 10: float32 [6, 512, 512], replicated
- output 11: float32 [6, 4, 512], replicated
All inputs are finite; a program needn't handle non-finite values.
Results may differ from a plain program's by a relative error of at most 0.0191016.
Values are sent between devices in bfloat16 or wider.
A program may use at most 1 GiB of HBM per device.

v0:
```python
import jax
import jax.numpy as jnp
from jax import lax
from jax.sharding import PartitionSpec as P

LN_EPS = 1e-5
AXIS_NAME = 'gp'


def matmul(lhs, rhs):
    return jnp.dot(lhs, rhs, preferred_element_type=jnp.float32)


def contract_rows(lhs, rhs):
    return lax.dot_general(lhs, rhs, (((0,), (0,)), ((), ())), preferred_element_type=jnp.float32)


def contract_cols(lhs, rhs):
    return lax.dot_general(lhs, rhs, (((1,), (1,)), ((), ())), preferred_element_type=jnp.float32)


def mlp_tail(pre_act, w_two, vec_rows):
    pre_bias = pre_act + vec_rows[0]
    hidden = jax.nn.silu(pre_bias).astype(jnp.bfloat16)
    out_lin = matmul(hidden, w_two) + vec_rows[1]
    centered = out_lin - jnp.mean(out_lin, axis=-1, keepdims=True)
    inv_std = lax.rsqrt(jnp.mean(centered * centered, axis=-1, keepdims=True) + LN_EPS)
    normed = centered * inv_std
    return normed * vec_rows[2] + vec_rows[3], (pre_bias, hidden, normed, inv_std)


def mlp_tail_back(saved, w_two, vec_rows, d_out):
    pre_bias, hidden, normed, inv_std = saved
    d_normed = d_out * vec_rows[2]
    d_lin = inv_std * (d_normed - jnp.mean(d_normed, axis=-1, keepdims=True) - normed * jnp.mean(d_normed * normed, axis=-1, keepdims=True))
    d_lin_bf = d_lin.astype(jnp.bfloat16)
    d_w_two = contract_rows(hidden, d_lin_bf)
    d_hidden = contract_cols(d_lin_bf, w_two)
    sig_pre = jax.nn.sigmoid(pre_bias)
    d_pre = d_hidden * sig_pre * (1.0 + pre_bias * (1.0 - sig_pre))
    d_vec = jnp.stack([jnp.sum(d_pre, axis=0), jnp.sum(d_lin, axis=0), jnp.sum(d_out * normed, axis=0), jnp.sum(d_out, axis=0)])
    return d_pre.astype(jnp.bfloat16), d_w_two, d_vec


def solution(mesh):
    row_spec = P(AXIS_NAME, None)
    edge_spec = P(AXIS_NAME)
    rep_spec = P()
    in_specs = (row_spec, row_spec, row_spec, row_spec, edge_spec, edge_spec) + (rep_spec,) * 8 + (row_spec, row_spec)
    out_specs = (row_spec, row_spec, row_spec) + (rep_spec,) * 8

    def local_step(grid_in, mesh_static, edge_static, send_rows, edge_src, edge_dst, w_grid_in, w_mesh_in, w_edge_in, w_edge_up, w_mesh_up, w_grid_up, w_second, vectors, d_mesh_out, d_grid_out):
        latent = w_grid_up.shape[0]
        grid_rows = grid_in.shape[0]
        mesh_rows = mesh_static.shape[0]
        slot_rows = send_rows.size
        send_flat = send_rows.reshape(-1)
        up_edge = w_edge_up[:latent]
        up_send = w_edge_up[latent:2 * latent]
        up_recv = w_edge_up[2 * latent:]
        node_self = w_mesh_up[:latent]
        node_agg = w_mesh_up[latent:]

        grid_emb, grid_save = mlp_tail(matmul(grid_in, w_grid_in), w_second[0], vectors[0])
        grid_lat = grid_emb.astype(jnp.bfloat16)
        mesh_emb, mesh_save = mlp_tail(matmul(mesh_static, w_mesh_in), w_second[1], vectors[1])
        mesh_lat = mesh_emb.astype(jnp.bfloat16)
        edge_emb, edge_save = mlp_tail(matmul(edge_static, w_edge_in), w_second[2], vectors[2])
        edge_lat = edge_emb.astype(jnp.bfloat16)

        outgoing = jnp.take(grid_lat, send_flat, axis=0)
        incoming = lax.all_to_all(outgoing, AXIS_NAME, 0, 0, tiled=True)

        edge_pre = (matmul(edge_lat, up_edge)
                    + jnp.take(matmul(incoming, up_send), edge_src, axis=0)
                    + jnp.take(matmul(mesh_lat, up_recv), edge_dst, axis=0))
        edge_upd, upd_save = mlp_tail(edge_pre, w_second[3], vectors[3])
        edge_new = (edge_lat.astype(jnp.float32) + edge_upd).astype(jnp.bfloat16)
        agg_sum = jax.ops.segment_sum(edge_new.astype(jnp.float32), edge_dst, num_segments=mesh_rows).astype(jnp.bfloat16)
        node_upd, node_save = mlp_tail(matmul(mesh_lat, node_self) + matmul(agg_sum, node_agg), w_second[4], vectors[4])
        mesh_out = (mesh_lat.astype(jnp.float32) + node_upd).astype(jnp.bfloat16)
        cell_upd, cell_save = mlp_tail(matmul(grid_lat, w_grid_up), w_second[5], vectors[5])
        grid_out = (grid_lat.astype(jnp.float32) + cell_upd).astype(jnp.bfloat16)

        d_grid_top = d_grid_out.astype(jnp.float32)
        d_mesh_top = d_mesh_out.astype(jnp.float32)
        d_pre5, d_two5, d_vec5 = mlp_tail_back(cell_save, w_second[5], vectors[5], d_grid_top)
        d_w_grid_up = contract_rows(grid_lat, d_pre5)
        d_grid_lat = d_grid_top + contract_cols(d_pre5, w_grid_up)
        d_pre4, d_two4, d_vec4 = mlp_tail_back(node_save, w_second[4], vectors[4], d_mesh_top)
        d_w_mesh_up = jnp.concatenate([contract_rows(mesh_lat, d_pre4), contract_rows(agg_sum, d_pre4)], axis=0)
        d_mesh_lat = d_mesh_top + contract_cols(d_pre4, node_self)
        d_agg = contract_cols(d_pre4, node_agg)
        d_edge_new = jnp.take(d_agg, edge_dst, axis=0)
        d_pre3, d_two3, d_vec3 = mlp_tail_back(upd_save, w_second[3], vectors[3], d_edge_new)
        d_pre3_wide = d_pre3.astype(jnp.float32)
        d_slot_pre = jax.ops.segment_sum(d_pre3_wide, edge_src, num_segments=slot_rows).astype(jnp.bfloat16)
        d_node_pre = jax.ops.segment_sum(d_pre3_wide, edge_dst, num_segments=mesh_rows).astype(jnp.bfloat16)
        d_w_edge_up = jnp.concatenate([contract_rows(edge_lat, d_pre3), contract_rows(incoming, d_slot_pre), contract_rows(mesh_lat, d_node_pre)], axis=0)
        d_edge_lat = d_edge_new + contract_cols(d_pre3, up_edge)
        d_mesh_lat = d_mesh_lat + contract_cols(d_node_pre, up_recv)
        d_incoming = contract_cols(d_slot_pre, up_send).astype(jnp.bfloat16)
        d_outgoing = lax.all_to_all(d_incoming, AXIS_NAME, 0, 0, tiled=True)
        d_grid_lat = d_grid_lat + jax.ops.segment_sum(d_outgoing.astype(jnp.float32), send_flat, num_segments=grid_rows)
        d_pre2, d_two2, d_vec2 = mlp_tail_back(edge_save, w_second[2], vectors[2], d_edge_lat)
        d_w_edge_in = contract_rows(edge_static, d_pre2)
        d_pre1, d_two1, d_vec1 = mlp_tail_back(mesh_save, w_second[1], vectors[1], d_mesh_lat)
        d_w_mesh_in = contract_rows(mesh_static, d_pre1)
        d_pre0, d_two0, d_vec0 = mlp_tail_back(grid_save, w_second[0], vectors[0], d_grid_lat)
        d_w_grid_in = contract_rows(grid_in, d_pre0)
        d_grid_in = contract_cols(d_pre0, w_grid_in)

        weight_grads = (d_w_grid_in, d_w_mesh_in, d_w_edge_in, d_w_edge_up, d_w_mesh_up, d_w_grid_up,
                        jnp.stack([d_two0, d_two1, d_two2, d_two3, d_two4, d_two5]),
                        jnp.stack([d_vec0, d_vec1, d_vec2, d_vec3, d_vec4, d_vec5]))
        weight_grads = lax.psum(weight_grads, AXIS_NAME)
        return (mesh_out, grid_out, d_grid_in) + weight_grads

    return jax.shard_map(local_step, mesh=mesh, in_specs=in_specs, out_specs=out_specs, check_vma=False)
```

profile of v0, /device:TPU:1, one launch (start us, length us, event | category | flops | bytes accessed | tf_op | source)
XLA Modules:
  0.0 433.5 jit_solution(7589507905270431873)
XLA Ops:
  9.9 1.6 convolution_add_fusion.10
  11.5 2.0 fusion.119
  14.2 2.0 gather_fusion
  17.2 7.8 %all-to-all-start = ((bf16[32,16,512]{2,1,0:T(8,128)(2,1)}), bf16[32,16,512]{2,1,0:T(8,128)(2,1)}, u32[]{:S(2)}, u32[]{:S(2)}) async-start(bf16[32,16,512]{2,1,0:T(8,128)(2,1)} %broadcast_select_fusion), calls=%async_computation | async-start | bytes 1048576 | tf_op jit(solution)/shard_map/all_to_all | solution.py:72
  27.3 2.0 fusion.118
  37.3 1.9 fusion.61
  39.6 2.1 copy.46
  41.6 2.6 copy.48
  44.2 3.1 gather_fusion.2
  47.3 2.7 fusion.96
  51.5 1.6 fusion.64
  53.1 3.1 gather_fusion.1
  56.2 3.4 fusion.4
  59.6 2.2 fusion.121
  63.8 1.7 fusion.32
  65.5 3.0 copy.42
  68.5 7.7 %scatter_custom_fusion = f32[512,512]{1,0:T(8,128)S(1)} fusion(s32[768]{0:T(1024)S(1)} %copy-done.65, f32[768,512]{1,0:T(8,128)} %copy.42, f32[]{:T(128)} %constant.63.clone.1), kind=kCustom, calls=%fused_computation.145 | custom fusion | flops 393216 | bytes 1049088 | tf_op jit(solution)/shard_map/scatter-add | solution.py:79
  76.2 1.8 fusion.19
  78.0 2.0 fusion.122
  80.6 2.0 fusion.115
  87.5 3.3 gather_fusion.3
  90.8 3.0 copy.47
  93.9 2.7 multiply_reduce_fusion
  98.1 2.2 fusion.114
  101.2 3.2 multiply_reduce_fusion.1
  104.4 7.5 %scatter_custom_fusion.3 = f32[512,512]{1,0:T(8,128)S(1)} fusion(s32[768]{0:T(1024)S(1)} %copy-done.65, bf16[768,512]{1,0:T(8,128)(2,1)} %copy-done.32, f32[]{:T(128)} %constant.63.clone.1), kind=kCustom, calls=%fused_computation.10 | custom fusion | flops 786432 | bytes 1835012 | tf_op jit(solution)/shard_map/scatter-add | solution.py:98
  111.9 8.4 %scatter_custom_fusion.1 = f32[512,512]{1,0:T(8,128)} fusion(s32[768]{0:T(1024)S(1)} %copy-done.66, bf16[768,512]{1,0:T(8,128)(2,1)} %copy-done.32, f32[]{:T(128)} %constant.63.clone.1), kind=kCustom, calls=%fused_computation.12 | custom fusion | flops 786432 | bytes 1835012 | tf_op jit(solution)/shard_map/scatter-add | solution.py:97
  120.3 3.1 fusion.91
  126.1 1.7 multiply_reduce_fusion.8
  127.8 5.9 %all-to-all-start.1 = ((bf16[32,16,512]{2,1,0:T(8,128)(2,1)}), bf16[32,16,512]{2,1,0:T(8,128)(2,1)}, u32[]{:S(2)}, u32[]{:S(2)}) async-start(bf16[32,16,512]{2,1,0:T(8,128)(2,1)} %bitcast.207), calls=%async_computation.1 | async-start | bytes 1048576 | tf_op jit(solution)/shard_map/all_to_all | solution.py:103
  133.8 2.9 pad_maximum_fusion.1
  139.7 2.0 pad_maximum_fusion
  141.7 6.9 %all-to-all-done.1 = bf16[32,16,512]{2,1,0:T(8,128)(2,1)} async-done(((bf16[32,16,512]{2,1,0:T(8,128)(2,1)}), bf16[32,16,512]{2,1,0:T(8,128)(2,1)}, u32[]{:S(2)}, u32[]{:S(2)}) %all-to-all-start.1) | async-done | bytes 524320 | tf_op jit(solution)/shard_map/all_to_all | solution.py:103
  148.6 6.3 %scatter_custom_fusion.2 = f32[512,512]{1,0:T(8,128)} fusion(f32[512,512]{1,0:T(8,128)} %copy.48, s32[512]{0:T(512)S(1)} %reshape.295, bf16[512,512]{1,0:T(8,128)(2,1)} %bitcast.74), kind=kCustom, calls=%fused_computation.98 | custom fusion | flops 524288 | bytes 1572864 | tf_op jit(solution)/shard_map/scatter-add | solution.py:104
  158.9 1.8 fusion.124
  165.5 1.6 fusion.21
  169.3 1.8 fusion.12
  171.1 1.8 fusion.11
  172.9 4.0 fusion.105
  176.9 2.2 copy.55
  179.0 2.0 copy.54
  181.1 2.3 fusion.126
  185.1 1.8 fusion.125
  187.2 41.7 %all-reduce = (f32[3,512]{1,0:T(4,128)}, f32[4,512]{1,0:T(4,128)}, f32[6,4,512]{2,1,0:T(4,128)}) all-reduce(f32[3,512]{1,0:T(4,128)S(1)} %convolution_bitcast_fusion.8, f32[4,512]{1,0:T(4,128)S(1)} %convolution_bitcast_fusion.7, f32[6,4,512]{2,1,0:T(4,128)S(1)} %constant_dynamic-update-slice_fusion), channel_id=1, replica_groups=mesh['gp'=32] {'gp'}, use_global_device_ids=true, to_apply=%region_27.29 | all-reduce | flops 15872 | bytes 126976 | tf_op jit(solution)/shard_map/psum | solution.py:116
  230.3 183.9 %all-reduce.4.cloned.1.call-done = (f32[474,512]{1,0:T(8,128)}, f32[1536,512]{1,0:T(8,128)}, f32[1024,512]{1,0:T(8,128)}, f32[512,512]{1,0:T(8,128)}, f32[6,512,512]{2,1,0:T(8,128)}) async-done(((f32[474,512]{1,0:T(8,128)}, f32[1536,512]{1,0:T(8,128)}, f32[1024,512]{1,0:T(8,128)}, f32[512,512]{1,0:T(8,128)}, f32[6,512,512]{2,1,0:T(8,128)}), (f32[474,512]{1,0:T(8,128)}, f32[1536,512]{1,0:T(8,128)}, ...) | async-done | bytes 13553680 | tf_op jit(solution)/shard_map/psum | solution.py:116
  414.2 2.4 copy.76
  416.6 4.0 copy.77
  423.5 2.7 copy.80
  (235 shorter events, 48.9 us)
Async XLA Ops:
  7.2 22.4 %copy-start = (bf16[512,512]{1,0:T(8,128)(2,1)S(1)}, bf16[512,512]{1,0:T(8,128)(2,1)}, u32[]{:S(2)}) copy-start(bf16[512,512]{1,0:T(8,128)(2,1)} %param.29) | copy-start | bytes 1572868
  11.5 2.0 copy-start.49
  14.0 2.2 copy-start.18
  16.2 8.8 %copy-start.65 = (s32[768]{0:T(1024)S(1)}, s32[768]{0:T(1024)}, u32[]{:S(2)}) copy-start(s32[768]{0:T(1024)} %param.23) | copy-start | bytes 9220
  16.2 9.7 %copy-start.66 = (s32[768]{0:T(1024)S(1)}, s32[768]{0:T(1024)}, u32[]{:S(2)}) copy-start(s32[768]{0:T(1024)} %param.22) | copy-start | bytes 9220
  16.2 9.7 %copy-start.62 = (bf16[512,512]{1,0:T(8,128)(2,1)S(1)}, bf16[512,512]{1,0:T(8,128)(2,1)}, u32[]{:S(2)}) copy-start(bf16[512,512]{1,0:T(8,128)(2,1)} %param.33) | copy-start | bytes 1572868
  16.2 10.7 %copy-start.64 = (bf16[512,3]{0,1:T(4,128)(2,1)S(1)}, bf16[512,3]{0,1:T(4,128)(2,1)}, u32[]{:S(2)}) copy-start(bf16[512,3]{0,1:T(4,128)(2,1)} %param.19) | copy-start | bytes 9220
  16.2 10.7 %copy-start.67 = (bf16[3,512]{1,0:T(4,128)(2,1)S(1)}, bf16[3,512]{1,0:T(4,128)(2,1)}, u32[]{:S(2)}) copy-start(bf16[3,512]{1,0:T(4,128)(2,1)} %param.25) | copy-start | bytes 9220
  17.2 34.3 %all-to-all-start = ((bf16[32,16,512]{2,1,0:T(8,128)(2,1)}), bf16[32,16,512]{2,1,0:T(8,128)(2,1)}, u32[]{:S(2)}, u32[]{:S(2)}) async-start(bf16[32,16,512]{2,1,0:T(8,128)(2,1)} %broadcast_select_fusion), calls=%async_computation | async-start | bytes 1048576 | tf_op jit(solution)/shard_map/all_to_all | solution.py:72
  27.3 2.0 copy-start.53
  27.3 2.3 copy-start.19
  29.4 2.3 copy-start.69
  30.1 3.0 copy-start.51
  34.0 1.9 copy-start.35
  37.1 2.1 copy-start.4
  37.3 2.1 copy-start.9
  47.3 2.8 copy-start.10
  47.3 2.8 copy-start.27
  59.6 2.2 copy-start.44
  61.8 2.0 copy-start.5
  78.0 2.6 copy-start.47
  78.0 2.3 copy-start.22
  80.1 2.6 copy-start.16
  93.9 2.7 copy-start.3
  93.9 2.8 copy-start.8
  97.4 2.9 copy-start.57
  98.1 3.1 copy-start.6
  120.3 3.1 copy-start.13
  120.3 3.1 copy-start.24
  127.8 6.0 %copy-start.29 = (f32[512,512]{1,0:T(8,128)S(1)}, f32[512,512]{1,0:T(8,128)}, u32[]{:S(2)}) copy-start(f32[512,512]{1,0:T(8,128)} %fusion.101) | copy-start | bytes 3145732
  127.8 20.8 %all-to-all-start.1 = ((bf16[32,16,512]{2,1,0:T(8,128)(2,1)}), bf16[32,16,512]{2,1,0:T(8,128)(2,1)}, u32[]{:S(2)}, u32[]{:S(2)}) async-start(bf16[32,16,512]{2,1,0:T(8,128)(2,1)} %bitcast.207), calls=%async_computation.1 | async-start | bytes 1048576 | tf_op jit(solution)/shard_map/all_to_all | solution.py:103
  133.7 280.5 %all-reduce.4.cloned.1.call-start = ((), (), s32[]{:S(2)}) async-start(), calls=%async_computation.2 | async-start | bytes 27131904 | tf_op jit(solution)/shard_map/psum | solution.py:116
  133.8 2.9 copy-start.7
  133.8 2.9 copy-start.33
  158.5 5.1 %copy-start.60 = (bf16[512,512]{0,1:T(8,128)(2,1)}, bf16[512,512]{0,1:T(8,128)(2,1)S(1)}, u32[]{:S(2)}) copy-start(bf16[512,512]{0,1:T(8,128)(2,1)S(1)} %get-tuple-element.72) | copy-start | bytes 1572868
  163.5 2.0 copy-start.59
  167.2 2.0 copy-start.48
  169.2 1.8 copy-start.15
  169.2 1.8 copy-start.21
  169.2 1.8 copy-start.52
  176.8 4.2 copy-start.42
  185.1 43.8 %copy-start.37 = (bf16[512,512]{1,0:T(8,128)(2,1)S(1)}, bf16[512,512]{1,0:T(8,128)(2,1)}, u32[]{:S(2)}) copy-start(bf16[512,512]{1,0:T(8,128)(2,1)} %copy-done.36) | copy-start | bytes 1572868
  185.1 43.8 %copy-start.39 = (bf16[474,512]{1,0:T(8,128)(2,1)S(1)}, bf16[474,512]{1,0:T(8,128)(2,1)}, u32[]{:S(2)}) copy-start(bf16[474,512]{1,0:T(8,128)(2,1)} %param.24) | copy-start | bytes 1456132
  414.2 6.4 %copy-start.34 = (f32[1024,512]{1,0:T(8,128)S(1)}, f32[1024,512]{1,0:T(8,128)}, u32[]{:S(2)}) copy-start(f32[1024,512]{1,0:T(8,128)} %get-tuple-element.160) | copy-start | bytes 6291460
  414.2 9.3 %slice-start = ((s8[6291456]{0:T(1024)(128)(4,1)}), s8[4194304]{0:T(1024)(128)(4,1)S(1)}, s32[]{:S(2)}) async-start(s8[6291456]{0:T(1024)(128)(4,1)} %bitcast.204), calls=%async_computation.3 | async-start | bytes 8388608
  416.6 6.9 %slice-start.1 = ((s8[6291456]{0:T(1024)(128)(4,1)}), s8[2097152]{0:T(1024)(128)(4,1)S(1)}, s32[]{:S(2)}) async-start(s8[6291456]{0:T(1024)(128)(4,1)} %bitcast.204), calls=%async_computation.4 | async-start | bytes 4194304
  420.6 2.0 copy-start.56
  423.5 2.7 copy-start.1
  (27 other events, 38.8 us)
Sparse Core Ops, SparseCore 0:
  173.0 241.1 all-reduce.3
where the time goes:
time: 440 us; the launch traced here: 434 us
  waiting for transfers between devices  191 us (43%)
  matrix products  66.9 us (15%)
  local copies, waits for them, and re-layouts  53 us (12%)
  other arithmetic  52 us (12%)
  blocking collectives  41.7 us (9%)
  between operations  15.4 us (4%)
  starting transfers between devices  13.7 us (3%)
    psum x1, waiting for transfers between devices, local_step(): weight_grads = lax.psum(weight_grads, AXIS_NAME)  184 us
    psum x1, blocking collectives, local_step(): weight_grads = lax.psum(weight_grads, AXIS_NAME)  41.7 us
    unnamed x154, local copies, waits for them, and re-layouts  29.1 us
    dot_general x15, matrix products, matmul(): return jnp.dot(lhs, rhs, preferred_element_type=jnp.float32)  22.6 us
    dot_general x15, matrix products, contract_rows(): lax.dot_general(lhs, rhs, (((0,), (0,)), ((), ())), preferred_element_typ...  22.3 us
    dot_general x13, matrix products, contract_cols(): lax.dot_general(lhs, rhs, (((1,), (1,)), ((), ())), preferred_element_typ...  22 us
  transfers between devices with their start and end apart: 3, of which 2 were waited for; matrix products, arithmetic and copies ran while one was open for 11% of the time, Pallas kernels for 0%

commit v1 on v0

v1 whole, which is shorter than its diff:
```python
import jax
import jax.numpy as jnp
from jax import lax
from jax.experimental import pallas as pl
from jax.experimental.pallas import tpu as pltpu
from jax.sharding import PartitionSpec as P

LN_EPS = 1e-5
AXIS_NAME = 'gp'
NCHUNK = 13
TILE = 256
LATENT = 512
F32 = jnp.float32
BF16 = jnp.bfloat16


def matmul(lhs, rhs):
    return jnp.dot(lhs, rhs, preferred_element_type=jnp.float32)


def contract_rows(lhs, rhs):
    return lax.dot_general(lhs, rhs, (((0,), (0,)), ((), ())), preferred_element_type=jnp.float32)


def contract_cols(lhs, rhs):
    return lax.dot_general(lhs, rhs, (((1,), (1,)), ((), ())), preferred_element_type=jnp.float32)


class Place:
    def __init__(self):
        self.p = lax.axis_index(AXIS_NAME)
        self.c = self.p % 2
        self.x = (self.p // 2) % 2
        self.y = (self.p // 4) % 2
        self.z = self.p // 8
        self.core_peer = self.p + 1 - 2 * self.c
        self.x_peer = self.p + 2 - 4 * self.x
        self.y_peer = self.p + 4 - 8 * self.y

    def z_peer(self, j):
        return self.p % 8 + ((self.z + 1 + j) % 4) * 8


class Reducer:
    def __init__(self, at, grads, out, r0, r1, r2, r3, send, recv):
        self.at = at
        self.grads, self.out = grads, out
        self.r0, self.r1, self.r2, self.r3 = r0, r1, r2, r3
        self.send, self.recv = send, recv

    def spot(self, k):
        at = self.at
        odd = k % 2
        d1 = at.x * (1 - odd) + at.y * odd
        d2 = at.y * (1 - odd) + at.x * odd
        p1 = at.x_peer * (1 - odd) + at.y_peer * odd
        p2 = at.y_peer * (1 - odd) + at.x_peer * odd
        return d1, d2, p1, p2

    def copies(self, s, k):
        at = self.at
        d1, d2, p1, p2 = self.spot(k)

        def make(src, dst, lane, dev):
            return pltpu.make_async_remote_copy(
                src_ref=src, dst_ref=dst, send_sem=self.send.at[k, lane], recv_sem=self.recv.at[k, lane],
                device_id=(dev,), device_id_type=pl.DeviceIdType.MESH)

        def rows(start, size):
            return pl.ds(pl.multiple_of(start, 64), size)

        row1 = at.c * 256 + d1 * 128
        row2 = row1 + d2 * 64
        if s == 0:
            return [make(self.grads.at[k, rows((1 - at.c) * 256, 256)], self.r0.at[k], 0, at.core_peer)]
        if s == 1:
            return [make(self.grads.at[k, rows(at.c * 256 + (1 - d1) * 128, 128)], self.r1.at[k], 1, p1)]
        if s == 2:
            return [make(self.grads.at[k, rows(row1 + (1 - d2) * 64, 64)], self.r2.at[k], 2, p2)]
        if s == 3:
            cols = [pl.ds(pl.multiple_of(((at.z + 1 + j) % 4) * 128, 128), 128) for j in range(3)]
            return [make(self.grads.at[k, rows(row2, 64), cols[j]], self.r3.at[k, j], 3 + j, at.z_peer(j)) for j in range(3)]
        if s == 4:
            part = self.out.at[k, rows(row2, 64), pl.ds(pl.multiple_of(at.z * 128, 128), 128)]
            return [make(part, part, 6 + j, at.z_peer(j)) for j in range(3)]
        if s == 5:
            part = self.out.at[k, rows(row2, 64)]
            return [make(part, part, 9, p2)]
        if s == 6:
            part = self.out.at[k, rows(row1, 128)]
            return [make(part, part, 10, p1)]
        part = self.out.at[k, rows(at.c * 256, 256)]
        return [make(part, part, 11, at.core_peer)]

    def start(self, s, k):
        for copy in self.copies(s, k):
            copy.start()

    def stage(self, s, k):
        at = self.at
        d1, d2, _, _ = self.spot(k)
        for copy in self.copies(s, k):
            copy.wait_recv()
        row1 = at.c * 256 + d1 * 128
        row2 = row1 + d2 * 64
        if s < 3:
            start, size, landed = ((at.c * 256, 256, self.r0), (row1, 128, self.r1), (row2, 64, self.r2))[s]

            @pl.loop(0, size // 64)
            def _(i):
                mine = (k, pl.ds(pl.multiple_of(start + i * 64, 64), 64))
                theirs = landed[k, pl.ds(pl.multiple_of(i * 64, 64), 64)]
                self.grads[mine] = (self.grads[mine].astype(F32) + theirs.astype(F32)).astype(BF16)
        elif s == 3:
            spot = (k, pl.ds(pl.multiple_of(row2, 64), 64), pl.ds(pl.multiple_of(at.z * 128, 128), 128))
            total = self.grads[spot].astype(F32)
            for j in range(3):
                total = total + self.r3[k, j].astype(F32)
            self.out[spot] = total.astype(BF16)
        if s < 7:
            self.start(s + 1, k)

    def drain(self, k):
        for s in range(8):
            for copy in self.copies(s, k):
                copy.wait_send()


class Progress:
    def __init__(self, red):
        self.red, self.now, self.due = red, 0, []

    def ready(self, k):
        self.red.start(0, k)
        self.due += [(self.now + 1 + s, k, s) for s in range(8)]

    def poll(self):
        self.now += 1
        for _, k, s in sorted(d for d in self.due if d[0] <= self.now):
            self.red.stage(s, k)
        self.due = [d for d in self.due if d[0] > self.now]

    def finish(self):
        while self.due:
            self.poll()


def rows_of(i, tile=TILE):
    return pl.ds(pl.multiple_of(i * tile, tile), tile)


def step_kernel(grid_in, mesh_static, edge_static, send_row, src_row, dst_row, w_grid_in, w_mesh_in, w_edge_in, w_edge_up,
                w_mesh_up, w_grid_up, w_second, vectors, d_mesh_out, d_grid_out,
                mesh_out, grid_out, d_grid_in, sums,
                grads, r0, r1, r2, r3, red_send, red_recv, a2a_send, a2a_recv,
                hid0, dsl0, nrm0, inv0, hid1, dsl1, nrm1, inv1, hid2, dsl2, nrm2, inv2, hid3, dsl3, nrm3, inv3,
                hid_s, dlin_s, dpre_s, dlin3, dpre3, dpre4,
                pick_send, pick_src, pick_dst, grid_lat, mesh_lat, cat, edge_new, agg, d_agg, d_edge,
                outgoing, incoming, d_incoming, d_outgoing, d_grid_lat, d_node, d_slot, misc):
    at = Place()
    n_dev = 32
    barrier = pltpu.get_barrier_semaphore()

    @pl.loop(1, n_dev)
    def _(r):
        pl.semaphore_signal(barrier, inc=1, device_id=((at.p + r) % n_dev,), device_id_type=pl.DeviceIdType.MESH)

    red = Reducer(at, grads, sums, r0, r1, r2, r3, red_send, red_recv)
    prog = Progress(red)

    def vec(k, j):
        return vectors[k, pl.ds(j, 1), :]

    def tail(k, pre, rows, hid):
        pre = pre + vec(k, 0)
        sig = jax.nn.sigmoid(pre)
        act = pre * sig
        hid_bf = act.astype(BF16)
        hid[rows, :] = hid_bf
        out_lin = matmul(hid_bf, w_second[k]) + vec(k, 1)
        centered = out_lin - jnp.mean(out_lin, axis=-1, keepdims=True)
        inv = lax.rsqrt(jnp.mean(centered * centered, axis=-1, keepdims=True) + LN_EPS)
        normed = centered * inv
        return normed * vec(k, 2) + vec(k, 3), sig + act * (1.0 - sig), normed, inv

    def tail_saved(k, pre, rows, saves):
        hid, dsl, nrm, inv_ref = saves
        out, slope, normed, inv = tail(k, pre, rows, hid)
        dsl[rows, :] = slope
        nrm[rows, :] = normed
        inv_ref[rows, :] = inv
        return out

    def tail_back(k, d_out, slope, normed, inv, rows, dlin, dpre):
        d_normed = d_out * vec(k, 2)
        d_lin = inv * (d_normed - jnp.mean(d_normed, axis=-1, keepdims=True)
                       - normed * jnp.mean(d_normed * normed, axis=-1, keepdims=True))
        d_lin_bf = d_lin.astype(BF16)
        dlin[rows, :] = d_lin_bf
        d_pre = contract_cols(d_lin_bf, w_second[k]) * slope
        d_pre_bf = d_pre.astype(BF16)
        dpre[rows, :] = d_pre_bf
        for j, term in enumerate((d_pre, d_lin, d_out * normed, d_out)):
            spot = pl.ds(481 + 4 * k + j, 1)
            misc[spot, :] = misc[spot, :] + jnp.sum(term, axis=0, keepdims=True)
        return d_pre_bf

    def tail_back_saved(k, d_out, rows, saves, dlin, dpre):
        _, dsl, nrm, inv_ref = saves
        return tail_back(k, d_out, dsl[rows, :], nrm[rows, :], inv_ref[rows, :], rows, dlin, dpre)

    def weight_grad(k, lhs, rhs, n_rows, first=0):
        @pl.loop(0, LATENT // TILE)
        def _(i):
            cols = pl.ds(pl.multiple_of(first + i * TILE, TILE), TILE)
            part = contract_rows(lhs[pl.ds(0, n_rows), cols], rhs[pl.ds(0, n_rows), :])
            grads[k, rows_of(i), :] = part.astype(BF16)

    def exchange(src, dst, lane, start):
        def copy(r):
            to = (at.p + r) % n_dev
            return pltpu.make_async_remote_copy(
                src_ref=src.at[pl.ds(pl.multiple_of(to * 16, 16), 16)], dst_ref=dst.at[pl.ds(pl.multiple_of(at.p * 16, 16), 16)],
                send_sem=a2a_send.at[lane, r], recv_sem=a2a_recv.at[lane, r],
                device_id=(to,), device_id_type=pl.DeviceIdType.MESH)

        if start:
            @pl.loop(1, n_dev)
            def _(r):
                copy(r).start()

            mine = pl.ds(pl.multiple_of(at.p * 16, 16), 16)
            dst[mine, :] = src[mine, :]
        else:
            @pl.loop(1, n_dev)
            def _(r):
                copy(r).wait()

    saves0 = (hid0, dsl0, nrm0, inv0)
    saves1 = (hid1, dsl1, nrm1, inv1)
    saves2 = (hid2, dsl2, nrm2, inv2)
    saves3 = (hid3, dsl3, nrm3, inv3)
    misc[pl.ds(472, 40), :] = jnp.zeros((40, LATENT), F32)

    @pl.loop(0, 2)
    def _(i):
        rows = rows_of(i)
        out = tail_saved(0, matmul(grid_in[rows, :], w_grid_in[...]), rows, saves0)
        grid_lat[rows, :] = out.astype(BF16)
        ids = lax.broadcasted_iota(jnp.int32, (TILE, LATENT), 0) + i * TILE
        pick_send[rows, :] = jnp.where(ids == send_row[...], 1.0, 0.0).astype(BF16)

    @pl.loop(0, 2)
    def _(i):
        rows = rows_of(i)
        outgoing[rows, :] = contract_rows(pick_send[:, rows], grid_lat[...]).astype(BF16)

    pl.semaphore_wait(barrier, n_dev - 1)
    exchange(outgoing, incoming, 0, True)

    @pl.loop(0, 2)
    def _(i):
        rows = rows_of(i)
        lat = grid_lat[rows, :]
        upd, slope, normed, inv = tail(5, matmul(lat, w_grid_up[...]), rows, hid_s)
        grid_out[rows, :] = (lat.astype(F32) + upd).astype(BF16)
        d_top = d_grid_out[rows, :].astype(F32)
        d_pre = tail_back(5, d_top, slope, normed, inv, rows, dlin_s, dpre_s)
        d_grid_lat[rows, :] = d_top + contract_cols(d_pre, w_grid_up[...])

    weight_grad(0, grid_lat, dpre_s, 512)
    prog.ready(0)
    weight_grad(1, hid_s, dlin_s, 512)
    prog.ready(1)

    @pl.loop(0, 2)
    def _(i):
        rows = rows_of(i)
        out = tail_saved(1, matmul(mesh_static[rows, :], w_mesh_in[...]), rows, saves1)
        mesh_lat[rows, :] = out.astype(BF16)
        ids = lax.broadcasted_iota(jnp.int32, (TILE, 768), 0) + i * TILE
        pick_src[rows, :] = jnp.where(ids == src_row[...], 1.0, 0.0).astype(BF16)
        pick_dst[rows, :] = jnp.where(ids == dst_row[...], 1.0, 0.0).astype(BF16)

    prog.poll()

    @pl.loop(0, 3)
    def _(i):
        rows = rows_of(i)
        out = tail_saved(2, matmul(edge_static[rows, :], w_edge_in[...]), rows, saves2)
        cat[rows, pl.ds(0, 512)] = out.astype(BF16)
        cat[rows, pl.ds(1024, 512)] = contract_rows(pick_dst[:, rows], mesh_lat[...]).astype(BF16)

    prog.poll()
    exchange(outgoing, incoming, 0, False)

    @pl.loop(0, 3)
    def _(i):
        rows = rows_of(i)
        cat[rows, pl.ds(512, 512)] = contract_rows(pick_src[:, rows], incoming[...]).astype(BF16)
        upd = tail_saved(3, matmul(cat[rows, :], w_edge_up[...]), rows, saves3)
        edge_new[rows, :] = (cat[rows, pl.ds(0, 512)].astype(F32) + upd).astype(BF16)

    prog.poll()

    @pl.loop(0, 2)
    def _(i):
        rows = rows_of(i)
        lat = mesh_lat[rows, :]
        agg_bf = matmul(pick_dst[rows, :], edge_new[...]).astype(BF16)
        agg[rows, :] = agg_bf
        pre = matmul(lat, w_mesh_up[pl.ds(0, 512), :]) + matmul(agg_bf, w_mesh_up[pl.ds(512, 512), :])
        upd, slope, normed, inv = tail(4, pre, rows, hid_s)
        mesh_out[rows, :] = (lat.astype(F32) + upd).astype(BF16)
        d_pre = tail_back(4, d_mesh_out[rows, :].astype(F32), slope, normed, inv, rows, dlin_s, dpre4)
        d_agg[rows, :] = contract_cols(d_pre, w_mesh_up[pl.ds(512, 512), :]).astype(BF16)

    prog.poll()

    @pl.loop(0, 3)
    def _(i):
        rows = rows_of(i)
        d_out = contract_rows(pick_dst[:, rows], d_agg[...])
        d_edge[rows, :] = d_out.astype(BF16)
        tail_back_saved(3, d_out, rows, saves3, dlin3, dpre3)

    prog.poll()

    @pl.loop(0, 2)
    def _(i):
        rows = rows_of(i)
        slot = matmul(pick_src[rows, :], dpre3[...]).astype(BF16)
        d_incoming[rows, :] = contract_cols(slot, w_edge_up[pl.ds(512, 512), :]).astype(BF16)

    exchange(d_incoming, d_outgoing, 1, True)
    weight_grad(2, mesh_lat, dpre4, 512)
    prog.ready(2)
    weight_grad(3, agg, dpre4, 512)
    prog.ready(3)
    weight_grad(4, hid_s, dlin_s, 512)
    prog.ready(4)
    prog.poll()
    for part in range(3):
        weight_grad(5 + part, cat, dpre3, 768, first=512 * part)
        prog.ready(5 + part)
    weight_grad(8, hid3, dlin3, 768)
    prog.ready(8)
    prog.poll()

    @pl.loop(0, 3)
    def _(i):
        rows = rows_of(i)
        d_out = d_edge[rows, :].astype(F32) + contract_cols(dpre3[rows, :], w_edge_up[pl.ds(0, 512), :])
        tail_back_saved(2, d_out, rows, saves2, dlin_s, dpre_s)

    weight_grad(9, hid2, dlin_s, 768)
    misc[pl.ds(477, 4), :] = contract_rows(edge_static[...], dpre_s[...])
    prog.ready(9)
    prog.poll()

    @pl.loop(0, 2)
    def _(i):
        rows = rows_of(i)
        node = matmul(pick_dst[rows, :], dpre3[...]).astype(BF16)
        d_out = (d_mesh_out[rows, :].astype(F32) + contract_cols(dpre4[rows, :], w_mesh_up[pl.ds(0, 512), :])
                 + contract_cols(node, w_edge_up[pl.ds(1024, 512), :]))
        tail_back_saved(1, d_out, rows, saves1, dlin_s, dpre_s)

    weight_grad(10, hid1, dlin_s, 512)
    misc[pl.ds(474, 3), :] = contract_rows(mesh_static[...], dpre_s[pl.ds(0, 512), :])
    prog.ready(10)
    prog.poll()
    exchange(d_incoming, d_outgoing, 1, False)

    @pl.loop(0, 2)
    def _(i):
        rows = rows_of(i)
        d_out = d_grid_lat[rows, :] + matmul(pick_send[rows, :], d_outgoing[...])
        d_pre = tail_back_saved(0, d_out, rows, saves0, dlin_s, dpre_s)
        d_grid_in[rows, :] = contract_cols(d_pre, w_grid_in[...])

    weight_grad(12, hid0, dlin_s, 512)
    prog.ready(12)
    misc[pl.ds(0, 474), :] = contract_rows(grid_in[...], dpre_s[pl.ds(0, 512), :])
    grads[11] = misc[...].astype(BF16)
    prog.ready(11)
    prog.finish()

    @pl.loop(0, NCHUNK)
    def _(k):
        red.drain(k)


def fused_step(*args):
    def f32(*shape):
        return pltpu.VMEM(shape, F32)

    def bf16(*shape):
        return pltpu.VMEM(shape, BF16)

    def saves(n):
        return [bf16(n, 512), f32(n, 512), f32(n, 512), f32(n, 1)]

    scratch = [
        bf16(NCHUNK, 512, 512), bf16(NCHUNK, 256, 512), bf16(NCHUNK, 128, 512), bf16(NCHUNK, 64, 512), bf16(NCHUNK, 3, 64, 128),
        pltpu.SemaphoreType.DMA((NCHUNK, 12)), pltpu.SemaphoreType.DMA((NCHUNK, 12)),
        pltpu.SemaphoreType.DMA((2, 32)), pltpu.SemaphoreType.DMA((2, 32)),
        *saves(512), *saves(512), *saves(768), *saves(768),
        bf16(768, 512), bf16(768, 512), bf16(768, 512), bf16(768, 512), bf16(768, 512), bf16(512, 512),
        bf16(512, 512), bf16(512, 768), bf16(512, 768), bf16(512, 512), bf16(512, 512), bf16(768, 1536), bf16(768, 512),
        bf16(512, 512), bf16(512, 512), bf16(768, 512),
        bf16(512, 512), bf16(512, 512), bf16(512, 512), bf16(512, 512), f32(512, 512), bf16(8, 512), bf16(8, 512), f32(512, 512),
    ]
    return pl.pallas_call(
        step_kernel,
        out_shape=[jax.ShapeDtypeStruct((512, 512), BF16), jax.ShapeDtypeStruct((512, 512), BF16),
                   jax.ShapeDtypeStruct((512, 474), F32), jax.ShapeDtypeStruct((NCHUNK, 512, 512), BF16)],
        in_specs=[pl.BlockSpec(memory_space=pltpu.VMEM)] * len(args),
        out_specs=[pl.BlockSpec(memory_space=pltpu.VMEM)] * 4,
        scratch_shapes=scratch,
        compiler_params=pltpu.CompilerParams(collective_id=0, has_side_effects=True, vmem_limit_bytes=67043328),
    )(*args)


def solution(mesh):
    row_spec = P(AXIS_NAME, None)
    edge_spec = P(AXIS_NAME)
    rep_spec = P()
    in_specs = (row_spec, row_spec, row_spec, row_spec, edge_spec, edge_spec) + (rep_spec,) * 8 + (row_spec, row_spec)
    out_specs = (row_spec, row_spec, row_spec) + (rep_spec,) * 8

    def local_step(grid_in, mesh_static, edge_static, send_rows, edge_src, edge_dst, *rest):
        mesh_out, grid_out, d_grid_in, total = fused_step(
            grid_in, mesh_static, edge_static, send_rows.reshape(1, -1), edge_src.reshape(1, -1), edge_dst.reshape(1, -1), *rest)
        misc = total[11]
        weight_sums = (misc[:474], misc[474:477], misc[477:481], total[5:8].reshape(1536, 512), total[2:4].reshape(1024, 512),
                       total[0], jnp.stack([total[k] for k in (12, 10, 9, 8, 4, 1)]), misc[481:505].reshape(6, 4, 512))
        return (mesh_out, grid_out, d_grid_in) + tuple(part.astype(F32) for part in weight_sums)

    return jax.shard_map(local_step, mesh=mesh, in_specs=in_specs, out_specs=out_specs, check_vma=False)
```

time: 440 us -> 155 us (0.35); the launches traced: 434 us -> 154 us
  waiting for transfers between devices: 191 us -> 0 us
  Pallas kernels: 0 us -> 122 us
  matrix products: 66.9 us -> 0 us
  blocking collectives: 41.7 us -> 0 us
  other arithmetic: 52 us -> 14.1 us
  local copies, waits for them, and re-layouts: 53 us -> 17 us
  between operations: 15.4 us -> 0.71 us
  starting transfers between devices: 13.7 us -> 0 us
    psum x1 -> x0, waiting for transfers between devices: 184 us -> none  [local_step(): weight_grads = lax.psum(weight_grads, AXIS_NAME)]
    pallas_call x0 -> x1, Pallas kernels: none -> 122 us  [fused_step(): pl.pallas_call(step_kernel, out_shape=[jax.ShapeDtypeStruct((512, 512), B...]
    dot_general x43 -> x0, matrix products: 66.9 us -> none  [the longest x15 22.6 us: matmul(): return jnp.dot(lhs, rhs, preferred_element_type=jnp.float32)]
    psum x1 -> x0, blocking collectives: 41.7 us -> none  [local_step(): weight_grads = lax.psum(weight_grads, AXIS_NAME)]
    scatter-add x4 -> x0, other arithmetic: 29.8 us -> none  [the longest x1 8.42 us: local_step(): jax.ops.segment_sum(d_pre3_wide, edge_src, num_segments=slot_rows)]
    unnamed x154 -> x20, local copies, waits for them, and re-layouts: 29.1 us -> 10.1 us
    gather x5 -> x0, local copies, waits for them, and re-layouts: 14.5 us -> none  [the longest x2 6.33 us: local_step(): d_edge_new = jnp.take(d_agg, edge_dst, axis=0)]
    all_to_all x2 -> x0, starting transfers between devices: 13.7 us -> none  [the longest x1 7.8 us: local_step(): incoming = lax.all_to_all(outgoing, AXIS_NAME, 0, 0, tiled=True)]
  transfers between devices with their start and end apart: 3 -> 0, of which waited for: 2 -> 0; matrix products, arithmetic and copies ran while one was open for 11% -> 0% of each run, Pallas kernels for 0% -> 0%
where the time goes in v1:
time: 155 us; the launch traced here: 154 us
  Pallas kernels  122 us (79%)
  local copies, waits for them, and re-layouts  17 us (11%)
  other arithmetic  14.1 us (9%)
    pallas_call x1, Pallas kernels, fused_step(): pl.pallas_call(step_kernel, out_shape=[jax.ShapeDtypeStruct((512, 512), B...  122 us
    convert_element_type x7, other arithmetic, local_step(): part.astype(F32)  12.9 us
    unnamed x20, local copies, waits for them, and re-layouts  10.1 us

profile of v1, /device:TPU:1, one launch (start us, length us, event | category | flops | bytes accessed | tf_op | source)
XLA Modules:
  0.0 154.2 jit_solution(2147035179587212314)
XLA Ops:
  0.6 1.3 reshape.54.src_row
  1.9 1.3 reshape.55.dst_row
  3.2 0.8 copy.32
  3.9 0.7 reshape.53.send_row
  4.6 1.5 copy.34.mesh_static
  6.1 1.5 copy.35.edge_static
  7.6 2.0 %copy.33.grid_in = bf16[512,474]{1,0:T(8,128)(2,1)} copy(bf16[512,474]{0,1:T(8,128)(2,1)} %param.16) | data formatting | bytes 970752 | tf_op args[0]
  9.7 122.3 %shard_map.239 = (bf16[512,512]{1,0:T(8,128)(2,1)}, bf16[512,512]{1,0:T(8,128)(2,1)}, f32[512,474]{1,0:T(8,128)}, bf16[13,512,512]{2,1,0:T(8,128)(2,1)}) custom-call(bf16[512,474]{1,0:T(8,128)(2,1)} %copy.33.grid_in, bf16[512,3]{1,0:T(8,128)(2,1)} %copy.34.mesh_static, bf16[768,4]{1,0:T(8,128)(2,1)} %copy.35.edge_static, s32[1,512]{1,0:T(1,128)} %reshape.53.send_row, ...), custom_call_target="tpu_custom_call" | custom-call | tf_op jit(solution)/shard_map/pallas_call | solution.py:414
  132.0 1.3 bitcast_convert_fusion.4
  133.3 1.3 bitcast_convert_fusion.5
  134.6 0.8 slice_convert_fusion
  135.4 0.6 reshape.62
  136.0 2.5 %copy.36 = f32[512,474]{0,1:T(8,128)} copy(f32[512,474]{1,0:T(8,128)} %get-tuple-element.32) | data formatting | bytes 1941504
  138.5 2.1 %bitcast_convert_fusion.3 = f32[474,512]{1,0:T(8,128)} fusion(bf16[13,512,512]{2,1,0:T(8,128)(2,1)} %get-tuple-element.18), kind=kLoop, calls=%fused_computation.9 | loop fusion | flops 242688 | bytes 1456128 | tf_op jit(solution)/shard_map/convert_element_type | solution.py:438
  140.6 0.0 slice-start
  140.6 1.4 slice.52
  142.1 1.7 %bitcast_convert_fusion.1 = f32[1024,512]{1,0:T(8,128)} fusion(bf16[2,512,512]{2,1,0:T(8,128)(2,1)S(1)} %slice.52), kind=kLoop, calls=%fused_computation.1 | loop fusion | flops 524288 | bytes 3145728 | tf_op jit(solution)/shard_map/convert_element_type | solution.py:438
  143.8 0.0 slice-start.1
  143.8 1.7 %slice.51 = bf16[3,512,512]{2,1,0:T(8,128)(2,1)S(1)} slice(bf16[13,512,512]{2,1,0:T(8,128)(2,1)} %get-tuple-element.18), slice={[5:8], [0:512], [0:512]} | slice | bytes 3145728 | tf_op jit(solution)/shard_map/slice | solution.py:436
  145.4 2.2 %bitcast_convert_fusion = f32[1536,512]{1,0:T(8,128)} fusion(bf16[3,512,512]{2,1,0:T(8,128)(2,1)S(1)} %slice.51), kind=kLoop, calls=%fused_computation | loop fusion | flops 786432 | bytes 4718592 | tf_op jit(solution)/shard_map/convert_element_type | solution.py:438
  147.6 0.0 slice-done
  147.6 0.0 slice-done.1
  147.9 1.1 slice_dynamic-update-slice_fusion
  149.0 0.0 copy-start.1
  149.0 0.0 copy-start
  149.0 3.6 %convert_element_type.57 = f32[6,512,512]{2,1,0:T(8,128)} convert(bf16[6,512,512]{2,1,0:T(8,128)(2,1)S(1)} %get-tuple-element.41) | non-fusion elementwise | flops 1572864 | bytes 9437184 | tf_op jit(solution)/shard_map/convert_element_type | solution.py:438
  152.6 0.0 copy-done.1
  152.6 0.8 copy.44
  153.4 0.0 copy-done
  153.4 0.8 copy.45
  (6 shorter events, 0.2 us)
Async XLA Ops:
  140.6 7.0 %slice-start = ((s8[6815744]{0:T(1024)(128)(4,1)}), s8[4194304]{0:T(1024)(128)(4,1)S(1)}, s32[]{:S(2)}) async-start(s8[6815744]{0:T(1024)(128)(4,1)} %bitcast.18), calls=%async_computation | async-start | bytes 8388608
  143.8 3.9 %slice-start.1 = ((s8[6815744]{0:T(1024)(128)(4,1)}), s8[2621440]{0:T(1024)(128)(4,1)S(1)}, s32[]{:S(2)}) async-start(s8[6815744]{0:T(1024)(128)(4,1)} %bitcast.18), calls=%async_computation.1 | async-start | bytes 5242880
  149.0 3.6 %copy-start.1 = (bf16[512,512]{1,0:T(8,128)(2,1)S(1)}, bf16[512,512]{1,0:T(8,128)(2,1)}, u32[]{:S(2)}) copy-start(bf16[512,512]{1,0:T(8,128)(2,1)} %get-tuple-element.54) | copy-start | bytes 1572868
  149.0 4.4 %copy-start = (bf16[512,512]{1,0:T(8,128)(2,1)S(1)}, bf16[512,512]{1,0:T(8,128)(2,1)}, u32[]{:S(2)}) copy-start(bf16[512,512]{1,0:T(8,128)(2,1)} %get-tuple-element.55) | copy-start | bytes 1572868

commit v2 on v1

--- a/solution.py
+++ b/solution.py
@@ -126,32 +126,56 @@
                 copy.wait_send()
 
 
+ORDER = (
+        (),
+        (),
+        (),
+        (),
+        (),
+        (0, 1, 16, 17),
+        (32, 33),
+        (),
+        (48,),
+        (),
+        (49,),
+        (),
+        (),
+        (),
+        (),
+        (2,),
+        (),
+        (3, 64, 4, 5),
+        (6,),
+        (7, 8, 9),
+        (18, 19, 80, 10, 20, 21),
+        (22, 65),
+        (),
+        (23, 24, 12, 11, 35, 25, 34, 36, 96, 38, 51, 112, 40, 26, 50, 37, 52, 27, 81, 54, 42, 39, 67, 56, 28, 66, 97,
+     41, 53, 113, 43, 68, 44, 83, 70, 82, 58, 84, 55, 72, 99, 98, 57, 86, 115, 69, 88, 114, 100, 59, 60, 116, 102, 74,
+     85, 71, 118, 73, 90, 104, 75, 87, 76, 120, 101, 89, 117, 106, 103, 91, 92, 122, 119, 105, 108, 121, 107, 124, 123),
+)
+
+
 class Progress:
     def __init__(self, red):
-        self.red, self.now, self.due = red, 0, []
+        self.red, self.point = red, 0
 
     def ready(self, k):
         self.red.start(0, k)
-        self.due += [(self.now + 1 + s, k, s) for s in range(8)]
 
     def poll(self):
-        self.now += 1
-        for _, k, s in sorted(d for d in self.due if d[0] <= self.now):
-            self.red.stage(s, k)
-        self.due = [d for d in self.due if d[0] > self.now]
-
-    def finish(self):
-        while self.due:
-            self.poll()
+        for code in ORDER[self.point]:
+            self.red.stage(code // 16, code % 16)
+        self.point += 1
 
 
 def rows_of(i, tile=TILE):
     return pl.ds(pl.multiple_of(i * tile, tile), tile)
 
 
-def step_kernel(grid_in, mesh_static, edge_static, send_row, src_row, dst_row, w_grid_in, w_mesh_in, w_edge_in, w_edge_up,
+def step_kernel(grid_t, mesh_t, edge_t, send_t, src_row, dst_row, w_grid_in, w_mesh_in, w_edge_in, w_edge_up,
                 w_mesh_up, w_grid_up, w_second, vectors, d_mesh_out, d_grid_out,
-                mesh_out, grid_out, d_grid_in, sums,
+                mesh_out, grid_out, d_grid_t, sums,
                 grads, r0, r1, r2, r3, red_send, red_recv, a2a_send, a2a_recv,
                 hid0, dsl0, nrm0, inv0, hid1, dsl1, nrm1, inv1, hid2, dsl2, nrm2, inv2, hid3, dsl3, nrm3, inv3,
                 hid_s, dlin_s, dpre_s, dlin3, dpre3, dpre4,
@@ -242,13 +266,36 @@
     saves3 = (hid3, dsl3, nrm3, inv3)
     misc[pl.ds(472, 40), :] = jnp.zeros((40, LATENT), F32)
 
+    def tiles(n):
+        def run(body):
+            prog.poll()
+
+            @pl.loop(0, n)
+            def _(i):
+                body(i, rows_of(i))
+        return run
+
+    slots = send_t[...]
+    spread = jnp.where(lax.broadcasted_iota(jnp.int32, (32, 512), 0) == lax.broadcasted_iota(jnp.int32, (32, 512), 1) // 16,
+                       1.0, 0.0).astype(BF16)
+    slots = (matmul((slots // 32).astype(F32).astype(BF16), spread) * 32.0
+             + matmul((slots % 32).astype(F32).astype(BF16), spread))
+    own = lax.broadcasted_iota(jnp.int32, (16, 512), 0) == lax.broadcasted_iota(jnp.int32, (16, 512), 1) % 16
+    send_row = jnp.sum(jnp.where(own, slots, 0.0), axis=0, keepdims=True)
+
+    def pick(row, i):
+        ids = lax.broadcasted_iota(jnp.int32, (TILE, row.shape[1]), 0) + i * TILE
+        return jnp.where(ids == row, 1.0, 0.0).astype(BF16)
+
+    send_ids = send_row.astype(jnp.int32)
+    for i in range(2):
+        pick_send[rows_of(i), :] = pick(send_ids, i)
+
     @pl.loop(0, 2)
     def _(i):
         rows = rows_of(i)
-        out = tail_saved(0, matmul(grid_in[rows, :], w_grid_in[...]), rows, saves0)
+        out = tail_saved(0, contract_rows(grid_t[:, rows], w_grid_in[...]), rows, saves0)
         grid_lat[rows, :] = out.astype(BF16)
-        ids = lax.broadcasted_iota(jnp.int32, (TILE, LATENT), 0) + i * TILE
-        pick_send[rows, :] = jnp.where(ids == send_row[...], 1.0, 0.0).astype(BF16)
 
     @pl.loop(0, 2)
     def _(i):
@@ -258,9 +305,8 @@
     pl.semaphore_wait(barrier, n_dev - 1)
     exchange(outgoing, incoming, 0, True)
 
-    @pl.loop(0, 2)
-    def _(i):
-        rows = rows_of(i)
+    @tiles(2)
+    def _(i, rows):
         lat = grid_lat[rows, :]
         upd, slope, normed, inv = tail(5, matmul(lat, w_grid_up[...]), rows, hid_s)
         grid_out[rows, :] = (lat.astype(F32) + upd).astype(BF16)
@@ -268,26 +314,24 @@
         d_pre = tail_back(5, d_top, slope, normed, inv, rows, dlin_s, dpre_s)
         d_grid_lat[rows, :] = d_top + contract_cols(d_pre, w_grid_up[...])
 
-    weight_grad(0, grid_lat, dpre_s, 512)
-    prog.ready(0)
-    weight_grad(1, hid_s, dlin_s, 512)
-    prog.ready(1)
-
-    @pl.loop(0, 2)
-    def _(i):
-        rows = rows_of(i)
-        out = tail_saved(1, matmul(mesh_static[rows, :], w_mesh_in[...]), rows, saves1)
+    def grad(k, *args, **kwargs):
+        prog.poll()
+        weight_grad(k, *args, **kwargs)
+        prog.ready(k)
+
+    grad(0, grid_lat, dpre_s, 512)
+    grad(1, hid_s, dlin_s, 512)
+
+    @tiles(2)
+    def _(i, rows):
+        out = tail_saved(1, contract_rows(mesh_t[:, rows], w_mesh_in[...]), rows, saves1)
         mesh_lat[rows, :] = out.astype(BF16)
-        ids = lax.broadcasted_iota(jnp.int32, (TILE, 768), 0) + i * TILE
-        pick_src[rows, :] = jnp.where(ids == src_row[...], 1.0, 0.0).astype(BF16)
-        pick_dst[rows, :] = jnp.where(ids == dst_row[...], 1.0, 0.0).astype(BF16)
-
-    prog.poll()
-
-    @pl.loop(0, 3)
-    def _(i):
-        rows = rows_of(i)
-        out = tail_saved(2, matmul(edge_static[rows, :], w_edge_in[...]), rows, saves2)
+        pick_src[rows, :] = pick(src_row[...], i)
+        pick_dst[rows, :] = pick(dst_row[...], i)
+
+    @tiles(3)
+    def _(i, rows):
+        out = tail_saved(2, contract_rows(edge_t[:, rows], w_edge_in[...]), rows, saves2)
         cat[rows, pl.ds(0, 512)] = out.astype(BF16)
         cat[rows, pl.ds(1024, 512)] = contract_rows(pick_dst[:, rows], mesh_lat[...]).astype(BF16)
 
@@ -301,11 +345,8 @@
         upd = tail_saved(3, matmul(cat[rows, :], w_edge_up[...]), rows, saves3)
         edge_new[rows, :] = (cat[rows, pl.ds(0, 512)].astype(F32) + upd).astype(BF16)
 
-    prog.poll()
-
-    @pl.loop(0, 2)
-    def _(i):
-        rows = rows_of(i)
+    @tiles(2)
+    def _(i, rows):
         lat = mesh_lat[rows, :]
         agg_bf = matmul(pick_dst[rows, :], edge_new[...]).astype(BF16)
         agg[rows, :] = agg_bf
@@ -315,60 +356,42 @@
         d_pre = tail_back(4, d_mesh_out[rows, :].astype(F32), slope, normed, inv, rows, dlin_s, dpre4)
         d_agg[rows, :] = contract_cols(d_pre, w_mesh_up[pl.ds(512, 512), :]).astype(BF16)
 
-    prog.poll()
-
-    @pl.loop(0, 3)
-    def _(i):
-        rows = rows_of(i)
+    @tiles(3)
+    def _(i, rows):
         d_out = contract_rows(pick_dst[:, rows], d_agg[...])
         d_edge[rows, :] = d_out.astype(BF16)
         tail_back_saved(3, d_out, rows, saves3, dlin3, dpre3)
 
-    prog.poll()
-
-    @pl.loop(0, 2)
-    def _(i):
-        rows = rows_of(i)
+    @tiles(2)
+    def _(i, rows):
         slot = matmul(pick_src[rows, :], dpre3[...]).astype(BF16)
         d_incoming[rows, :] = contract_cols(slot, w_edge_up[pl.ds(512, 512), :]).astype(BF16)
 
     exchange(d_incoming, d_outgoing, 1, True)
-    weight_grad(2, mesh_lat, dpre4, 512)
-    prog.ready(2)
-    weight_grad(3, agg, dpre4, 512)
-    prog.ready(3)
-    weight_grad(4, hid_s, dlin_s, 512)
-    prog.ready(4)
-    prog.poll()
+    grad(2, mesh_lat, dpre4, 512)
+    grad(3, agg, dpre4, 512)
+    grad(4, hid_s, dlin_s, 512)
     for part in range(3):
-        weight_grad(5 + part, cat, dpre3, 768, first=512 * part)
-        prog.ready(5 + part)
-    weight_grad(8, hid3, dlin3, 768)
-    prog.ready(8)
-    prog.poll()
-
-    @pl.loop(0, 3)
-    def _(i):
-        rows = rows_of(i)
+        grad(5 + part, cat, dpre3, 768, first=512 * part)
+    grad(8, hid3, dlin3, 768)
+
+    @tiles(3)
+    def _(i, rows):
         d_out = d_edge[rows, :].astype(F32) + contract_cols(dpre3[rows, :], w_edge_up[pl.ds(0, 512), :])
         tail_back_saved(2, d_out, rows, saves2, dlin_s, dpre_s)
 
-    weight_grad(9, hid2, dlin_s, 768)
-    misc[pl.ds(477, 4), :] = contract_rows(edge_static[...], dpre_s[...])
-    prog.ready(9)
-    prog.poll()
-
-    @pl.loop(0, 2)
-    def _(i):
-        rows = rows_of(i)
+    misc[pl.ds(477, 4), :] = matmul(edge_t[...], dpre_s[...])
+    grad(9, hid2, dlin_s, 768)
+
+    @tiles(2)
+    def _(i, rows):
         node = matmul(pick_dst[rows, :], dpre3[...]).astype(BF16)
         d_out = (d_mesh_out[rows, :].astype(F32) + contract_cols(dpre4[rows, :], w_mesh_up[pl.ds(0, 512), :])
                  + contract_cols(node, w_edge_up[pl.ds(1024, 512), :]))
         tail_back_saved(1, d_out, rows, saves1, dlin_s, dpre_s)
 
-    weight_grad(10, hid1, dlin_s, 512)
-    misc[pl.ds(474, 3), :] = contract_rows(mesh_static[...], dpre_s[pl.ds(0, 512), :])
-    prog.ready(10)
+    misc[pl.ds(474, 3), :] = matmul(mesh_t[...], dpre_s[pl.ds(0, 512), :])
+    grad(10, hid1, dlin_s, 512)
     prog.poll()
     exchange(d_incoming, d_outgoing, 1, False)
 
@@ -377,14 +400,14 @@
         rows = rows_of(i)
         d_out = d_grid_lat[rows, :] + matmul(pick_send[rows, :], d_outgoing[...])
         d_pre = tail_back_saved(0, d_out, rows, saves0, dlin_s, dpre_s)
-        d_grid_in[rows, :] = contract_cols(d_pre, w_grid_in[...])
-
-    weight_grad(12, hid0, dlin_s, 512)
-    prog.ready(12)
-    misc[pl.ds(0, 474), :] = contract_rows(grid_in[...], dpre_s[pl.ds(0, 512), :])
+        d_grid_t[:, rows] = contract_cols(w_grid_in[...], d_pre)
+
+    grad(12, hid0, dlin_s, 512)
+    prog.poll()
+    misc[pl.ds(0, 474), :] = matmul(grid_t[...], dpre_s[pl.ds(0, 512), :])
     grads[11] = misc[...].astype(BF16)
     prog.ready(11)
-    prog.finish()
+    prog.poll()
 
     @pl.loop(0, NCHUNK)
     def _(k):
@@ -414,12 +437,75 @@
     return pl.pallas_call(
         step_kernel,
         out_shape=[jax.ShapeDtypeStruct((512, 512), BF16), jax.ShapeDtypeStruct((512, 512), BF16),
-                   jax.ShapeDtypeStruct((512, 474), F32), jax.ShapeDtypeStruct((NCHUNK, 512, 512), BF16)],
+                   jax.ShapeDtypeStruct((474, 512), F32), jax.ShapeDtypeStruct((NCHUNK, 512, 512), BF16)],
         in_specs=[pl.BlockSpec(memory_space=pltpu.VMEM)] * len(args),
         out_specs=[pl.BlockSpec(memory_space=pltpu.VMEM)] * 4,
         scratch_shapes=scratch,
         compiler_params=pltpu.CompilerParams(collective_id=0, has_side_effects=True, vmem_limit_bytes=67043328),
     )(*args)
+
+
+HOME = {0: (2, 0), 1: (3, 5), 2: (1, 0), 3: (1, 1), 4: (3, 4), 5: (0, 0), 6: (0, 1), 7: (0, 2), 8: (3, 3), 9: (3, 2), 10: (3, 1), 12: (3, 0)}
+
+
+def spread_kernel(mesh_in, grid_in, d_grid_in, sums, mesh_out, grid_out, d_grid_out, edge_up, mesh_up, grid_up, second,
+                  w_grid, w_mesh, w_edge, vecs, mesh_buf, grid_buf, d_grid_buf, sum_buf, wide, sem_in, sem_out):
+    loads = [pltpu.make_async_copy(sums.at[k], sum_buf.at[k], sem_in.at[k]) for k in range(NCHUNK)]
+    through = [(mesh_in, mesh_buf, mesh_out), (grid_in, grid_buf, grid_out), (d_grid_in, d_grid_buf, d_grid_out)]
+    heads = [pltpu.make_async_copy(a, b, sem_in.at[NCHUNK + i]) for i, (a, b, _) in enumerate(through)]
+    tails = [pltpu.make_async_copy(b, c, sem_out.at[NCHUNK + i]) for i, (_, b, c) in enumerate(through)]
+    loads[11].start()
+    for k in range(NCHUNK):
+        if k != 11:
+            loads[k].start()
+    for copy in heads:
+        copy.start()
+    outs = (edge_up, mesh_up, grid_up, second)
+    stores = []
+    loads[11].wait()
+    misc = sum_buf[11].astype(F32)
+    w_grid[...] = misc[:474]
+    w_mesh[...] = misc[474:477]
+    w_edge[...] = misc[477:481]
+    for k in range(6):
+        vecs[k] = misc[481 + 4 * k:485 + 4 * k]
+    for k, (out, part) in HOME.items():
+        loads[k].wait()
+
+        @pl.loop(0, 8)
+        def _(i):
+            rows = rows_of(i, 64)
+            wide[k, rows, :] = sum_buf[k, rows, :].astype(F32)
+
+        home = outs[out].at[part] if out == 3 else outs[out].at[pl.ds(part * 512, 512)]
+        stores.append(pltpu.make_async_copy(wide.at[k], home, sem_out.at[k]))
+        stores[-1].start()
+    for head, tail in zip(heads, tails):
+        head.wait()
+        tail.start()
+    for copy in stores + tails:
+        copy.wait()
+
+
+def spread_out(*parts):
+    def out(dtype, *shape):
+        return jax.ShapeDtypeStruct(shape, dtype)
+
+    anywhere = pl.BlockSpec(memory_space=pl.ANY)
+    here = pl.BlockSpec(memory_space=pltpu.VMEM)
+    mesh_out, grid_out, d_grid, edge_up, mesh_up, grid_up, second, w_grid, w_mesh, w_edge, vecs = pl.pallas_call(
+        spread_kernel,
+        out_shape=[out(BF16, 512, 512), out(BF16, 512, 512), out(F32, 474, 512), out(F32, 1536, 512), out(F32, 1024, 512),
+                   out(F32, 512, 512), out(F32, 6, 512, 512), out(F32, 474, 512), out(F32, 3, 512), out(F32, 4, 512),
+                   out(F32, 6, 4, 512)],
+        in_specs=[anywhere] * 4,
+        out_specs=[anywhere] * 7 + [here] * 4,
+        scratch_shapes=[pltpu.VMEM((512, 512), BF16), pltpu.VMEM((512, 512), BF16), pltpu.VMEM((474, 512), F32),
+                        pltpu.VMEM((NCHUNK, 512, 512), BF16), pltpu.VMEM((NCHUNK, 512, 512), F32),
+                        pltpu.SemaphoreType.DMA((NCHUNK + 3,)), pltpu.SemaphoreType.DMA((NCHUNK + 3,))],
+        compiler_params=pltpu.CompilerParams(vmem_limit_bytes=48 * 2**20),
+    )(*parts)
+    return mesh_out, grid_out, d_grid, w_grid, w_mesh, w_edge, edge_up, mesh_up, grid_up, second, vecs
 
 
 def solution(mesh):
@@ -430,11 +516,9 @@
     out_specs = (row_spec, row_spec, row_spec) + (rep_spec,) * 8
 
     def local_step(grid_in, mesh_static, edge_static, send_rows, edge_src, edge_dst, *rest):
-        mesh_out, grid_out, d_grid_in, total = fused_step(
-            grid_in, mesh_static, edge_static, send_rows.reshape(1, -1), edge_src.reshape(1, -1), edge_dst.reshape(1, -1), *rest)
-        misc = total[11]
-        weight_sums = (misc[:474], misc[474:477], misc[477:481], total[5:8].reshape(1536, 512), total[2:4].reshape(1024, 512),
-                       total[0], jnp.stack([total[k] for k in (12, 10, 9, 8, 4, 1)]), misc[481:505].reshape(6, 4, 512))
-        return (mesh_out, grid_out, d_grid_in) + tuple(part.astype(F32) for part in weight_sums)
+        parts = fused_step(grid_in.T, mesh_static.T, edge_static.T, send_rows.T,
+                           edge_src.reshape(1, -1), edge_dst.reshape(1, -1), *rest)
+        mesh_out, grid_out, d_grid_t, *sums = spread_out(*parts)
+        return (mesh_out, grid_out, d_grid_t.T) + tuple(sums)
 
     return jax.shard_map(local_step, mesh=mesh, in_specs=in_specs, out_specs=out_specs, check_vma=False)

time: 155 us -> 130 us (0.84)
  other arithmetic: 14.1 us -> 0 us
  local copies, waits for them, and re-layouts: 17 us -> 5.81 us
    convert_element_type x7 -> x0, other arithmetic: 12.9 us -> none  [local_step(): part.astype(F32)]
    pallas_call x0 -> x1, Pallas kernels: none -> 7.94 us  [spread_out(): pl.pallas_call(spread_kernel, out_shape=[out(BF16, 512, 512), out(BF16, 5...]
    pallas_call x1, Pallas kernels: 122 us -> 115 us  [fused_step(): pl.pallas_call(step_kernel, out_shape=[jax.ShapeDtypeStruct((512, 512), B...]
    unnamed x20 -> x6, local copies, waits for them, and re-layouts: 10.1 us -> 3.28 us
    slice x2 -> x0, local copies, waits for them, and re-layouts: 3.1 us -> none  [the longest x1 1.66 us: local_step(): total[5:8].reshape(1536, 512)]
where the time goes in v2:
time: 130 us
  Pallas kernels  123 us (95%)
  local copies, waits for them, and re-layouts  5.81 us (4%)
    pallas_call x1, Pallas kernels, fused_step(): pl.pallas_call(step_kernel, out_shape=[jax.ShapeDtypeStruct((512, 512), B...  115 us
    pallas_call x1, Pallas kernels, spread_out(): pl.pallas_call(spread_kernel, out_shape=[out(BF16, 512, 512), out(BF16, 5...  7.94 us
    unnamed x6, local copies, waits for them, and re-layouts  3.28 us

profile of v2, /device:TPU:1, one launch (start us, length us, event | category | flops | bytes accessed | tf_op | source)
XLA Modules:
  0.0 129.7 jit_solution(636107829760629819)
XLA Ops:
  0.6 1.3 reshape.28.src_row
  1.9 1.3 reshape.29.dst_row
  3.2 115.3 %shard_map.239 = (bf16[512,512]{1,0:T(8,128)(2,1)}, bf16[512,512]{1,0:T(8,128)(2,1)}, f32[474,512]{1,0:T(8,128)}, bf16[13,512,512]{2,1,0:T(8,128)(2,1)}) custom-call(bf16[474,512]{1,0:T(8,128)(2,1)} %bitcast.5, bf16[3,512]{1,0:T(4,128)(2,1)} %bitcast.8, bf16[4,768]{1,0:T(4,128)(2,1)} %bitcast.7, s32[16,32]{1,0:T(8,128)} %bitcast.6, ...), custom_call_target="tpu_custom_call" | custom-call | tf_op jit(solution)/shard_map/pallas_call | solution.py:437
  118.5 0.0 copy-start
  118.5 1.2 copy-done
  119.7 0.0 copy-start.1
  119.7 1.0 copy-done.1
  120.7 0.0 copy-start.2
  120.7 1.0 copy-done.2
  121.8 7.9 %shard_map.240 = (bf16[512,512]{1,0:T(8,128)(2,1)}, bf16[512,512]{1,0:T(8,128)(2,1)}, f32[474,512]{1,0:T(8,128)}, f32[1536,512]{1,0:T(8,128)}, f32[1024,512]{1,0...) custom-call(bf16[512,512]{1,0:T(8,128)(2,1)S(1)} %copy-done.1, ...), custom_call_target="tpu_custom_call" | custom-call | tf_op jit(solution)/shard_map/pallas_call | solution.py:496
Async XLA Ops:
  118.5 1.2 copy-start
  119.7 1.0 copy-start.1
  120.7 1.0 copy-start.2

commit v3 on v2

--- a/solution.py
+++ b/solution.py
@@ -131,34 +131,34 @@
         (),
         (),
         (),
-        (),
-        (0, 1, 16, 17),
-        (32, 33),
-        (),
-        (48,),
-        (),
-        (49,),
-        (),
-        (),
-        (),
-        (),
+        (0, 1),
+        (16, 17),
+        (32,),
+        (),
+        (),
+        (),
+        (),
+        (),
+        (),
+        (),
+        (33,),
         (2,),
-        (),
-        (3, 64, 4, 5),
-        (6,),
-        (7, 8, 9),
-        (18, 19, 80, 10, 20, 21),
-        (22, 65),
-        (),
-        (23, 24, 12, 11, 35, 25, 34, 36, 96, 38, 51, 112, 40, 26, 50, 37, 52, 27, 81, 54, 42, 39, 67, 56, 28, 66, 97,
-     41, 53, 113, 43, 68, 44, 83, 70, 82, 58, 84, 55, 72, 99, 98, 57, 86, 115, 69, 88, 114, 100, 59, 60, 116, 102, 74,
-     85, 71, 118, 73, 90, 104, 75, 87, 76, 120, 101, 89, 117, 106, 103, 91, 92, 122, 119, 105, 108, 121, 107, 124, 123),
+        (48, 3),
+        (4, 5),
+        (19, 6, 18),
+        (8, 20),
+        (49, 34, 7, 21),
+        (64, 35),
+        (22, 9, 65, 36, 10),
+        (37, 23, 80, 50, 24, 81, 12, 38, 51, 11, 25, 52, 26, 39, 53, 97, 40, 66, 96, 68, 67, 54, 27, 55, 41, 42, 112,
+     69, 28, 113, 82, 70, 83, 56, 43, 44, 85, 84, 57, 71, 98, 58, 100, 86, 72, 59, 87, 99, 114, 60, 101, 73, 74, 88,
+     116, 115, 102, 75, 89, 76, 90, 117, 103, 104, 91, 105, 92, 119, 106, 121, 120, 107, 118, 108, 122, 123, 124),
 )
 
 
 class Progress:
-    def __init__(self, red):
-        self.red, self.point = red, 0
+    def __init__(self, red, stores):
+        self.red, self.stores, self.point = red, stores, 0
 
     def ready(self, k):
         self.red.start(0, k)
@@ -166,6 +166,8 @@
     def poll(self):
         for code in ORDER[self.point]:
             self.red.stage(code // 16, code % 16)
+            if code // 16 == 7:
+                self.stores[code % 16].start()
         self.point += 1
 
 
@@ -173,9 +175,11 @@
     return pl.ds(pl.multiple_of(i * tile, tile), tile)
 
 
-def step_kernel(grid_t, mesh_t, edge_t, send_t, src_row, dst_row, w_grid_in, w_mesh_in, w_edge_in, w_edge_up,
-                w_mesh_up, w_grid_up, w_second, vectors, d_mesh_out, d_grid_out,
-                mesh_out, grid_out, d_grid_t, sums,
+def step_kernel(grid_h, mesh_t, edge_t, send_t, src_row, dst_row, w_grid_in_h, w_mesh_in, w_edge_in, w_edge_up_h,
+                w_mesh_up_h, w_grid_up_h, w_second_h, vectors, d_mesh_out_h, d_grid_out_h,
+                mesh_out_h, grid_out_h, d_grid_h, sums_h,
+                grid_t, w_grid_in, w_edge_up, w_mesh_up, w_grid_up, w_second, d_mesh_out, d_grid_out,
+                mesh_out, grid_out, d_grid_t, sums, load_sem, store_sem,
                 grads, r0, r1, r2, r3, red_send, red_recv, a2a_send, a2a_recv,
                 hid0, dsl0, nrm0, inv0, hid1, dsl1, nrm1, inv1, hid2, dsl2, nrm2, inv2, hid3, dsl3, nrm3, inv3,
                 hid_s, dlin_s, dpre_s, dlin3, dpre3, dpre4,
@@ -183,6 +187,21 @@
                 outgoing, incoming, d_incoming, d_outgoing, d_grid_lat, d_node, d_slot, misc):
     at = Place()
     n_dev = 32
+    moves = [(grid_h, grid_t), (w_grid_in_h, w_grid_in), (w_second_h.at[0], w_second.at[0]), (w_grid_up_h, w_grid_up),
+             (w_second_h.at[5], w_second.at[5]), (d_grid_out_h, d_grid_out), (w_second_h.at[1], w_second.at[1]),
+             (w_second_h.at[2], w_second.at[2]), (w_edge_up_h, w_edge_up), (w_second_h.at[3], w_second.at[3]),
+             (w_mesh_up_h, w_mesh_up), (w_second_h.at[4], w_second.at[4]), (d_mesh_out_h, d_mesh_out)]
+    loads = [pltpu.make_async_copy(src, dst, load_sem.at[i]) for i, (src, dst) in enumerate(moves)]
+    for copy in loads:
+        copy.start()
+    stores = [pltpu.make_async_copy(sums.at[k], sums_h.at[k], store_sem.at[k]) for k in range(NCHUNK)]
+    stores += [pltpu.make_async_copy(src, dst, store_sem.at[NCHUNK + i]) for i, (src, dst) in enumerate(
+        [(mesh_out, mesh_out_h), (grid_out, grid_out_h), (d_grid_t, d_grid_h)])]
+
+    def loaded(first, last):
+        for copy in loads[first:last]:
+            copy.wait()
+
     barrier = pltpu.get_barrier_semaphore()
 
     @pl.loop(1, n_dev)
@@ -190,7 +209,7 @@
         pl.semaphore_signal(barrier, inc=1, device_id=((at.p + r) % n_dev,), device_id_type=pl.DeviceIdType.MESH)
 
     red = Reducer(at, grads, sums, r0, r1, r2, r3, red_send, red_recv)
-    prog = Progress(red)
+    prog = Progress(red, stores)
 
     def vec(k, j):
         return vectors[k, pl.ds(j, 1), :]
@@ -291,6 +310,8 @@
     for i in range(2):
         pick_send[rows_of(i), :] = pick(send_ids, i)
 
+    loaded(0, 3)
+
     @pl.loop(0, 2)
     def _(i):
         rows = rows_of(i)
@@ -304,6 +325,7 @@
 
     pl.semaphore_wait(barrier, n_dev - 1)
     exchange(outgoing, incoming, 0, True)
+    loaded(3, 6)
 
     @tiles(2)
     def _(i, rows):
@@ -319,6 +341,8 @@
         weight_grad(k, *args, **kwargs)
         prog.ready(k)
 
+    stores[NCHUNK + 1].start()
+    loaded(6, 13)
     grad(0, grid_lat, dpre_s, 512)
     grad(1, hid_s, dlin_s, 512)
 
@@ -326,8 +350,8 @@
     def _(i, rows):
         out = tail_saved(1, contract_rows(mesh_t[:, rows], w_mesh_in[...]), rows, saves1)
         mesh_lat[rows, :] = out.astype(BF16)
-        pick_src[rows, :] = pick(src_row[...], i)
-        pick_dst[rows, :] = pick(dst_row[...], i)
+        pick_src[rows, :] = pick(src_row[...].reshape(1, 768), i)
+        pick_dst[rows, :] = pick(dst_row[...].reshape(1, 768), i)
 
     @tiles(3)
     def _(i, rows):
@@ -368,6 +392,7 @@
         d_incoming[rows, :] = contract_cols(slot, w_edge_up[pl.ds(512, 512), :]).astype(BF16)
 
     exchange(d_incoming, d_outgoing, 1, True)
+    stores[NCHUNK].start()
     grad(2, mesh_lat, dpre4, 512)
     grad(3, agg, dpre4, 512)
     grad(4, hid_s, dlin_s, 512)
@@ -402,6 +427,7 @@
         d_pre = tail_back_saved(0, d_out, rows, saves0, dlin_s, dpre_s)
         d_grid_t[:, rows] = contract_cols(w_grid_in[...], d_pre)
 
+    stores[NCHUNK + 2].start()
     grad(12, hid0, dlin_s, 512)
     prog.poll()
     misc[pl.ds(0, 474), :] = matmul(grid_t[...], dpre_s[pl.ds(0, 512), :])
@@ -413,6 +439,9 @@
     def _(k):
         red.drain(k)
 
+    for copy in stores:
+        copy.wait()
+
 
 def fused_step(*args):
     def f32(*shape):
@@ -425,6 +454,9 @@
         return [bf16(n, 512), f32(n, 512), f32(n, 512), f32(n, 1)]
 
     scratch = [
+        bf16(474, 512), bf16(474, 512), bf16(1536, 512), bf16(1024, 512), bf16(512, 512), bf16(6, 512, 512), bf16(512, 512),
+        bf16(512, 512), bf16(512, 512), bf16(512, 512), f32(474, 512), bf16(NCHUNK, 512, 512),
+        pltpu.SemaphoreType.DMA((13,)), pltpu.SemaphoreType.DMA((NCHUNK + 3,)),
         bf16(NCHUNK, 512, 512), bf16(NCHUNK, 256, 512), bf16(NCHUNK, 128, 512), bf16(NCHUNK, 64, 512), bf16(NCHUNK, 3, 64, 128),
         pltpu.SemaphoreType.DMA((NCHUNK, 12)), pltpu.SemaphoreType.DMA((NCHUNK, 12)),
         pltpu.SemaphoreType.DMA((2, 32)), pltpu.SemaphoreType.DMA((2, 32)),
@@ -438,8 +470,9 @@
         step_kernel,
         out_shape=[jax.ShapeDtypeStruct((512, 512), BF16), jax.ShapeDtypeStruct((512, 512), BF16),
                    jax.ShapeDtypeStruct((474, 512), F32), jax.ShapeDtypeStruct((NCHUNK, 512, 512), BF16)],
-        in_specs=[pl.BlockSpec(memory_space=pltpu.VMEM)] * len(args),
-        out_specs=[pl.BlockSpec(memory_space=pltpu.VMEM)] * 4,
+        in_specs=[pl.BlockSpec(memory_space=pltpu.HBM if i in (0, 6, 9, 10, 11, 12, 14, 15) else pltpu.VMEM)
+                  for i in range(len(args))],
+        out_specs=[pl.BlockSpec(memory_space=pltpu.HBM)] * 4,
         scratch_shapes=scratch,
         compiler_params=pltpu.CompilerParams(collective_id=0, has_side_effects=True, vmem_limit_bytes=67043328),
     )(*args)
@@ -491,7 +524,7 @@
     def out(dtype, *shape):
         return jax.ShapeDtypeStruct(shape, dtype)
 
-    anywhere = pl.BlockSpec(memory_space=pl.ANY)
+    anywhere = pl.BlockSpec(memory_space=pltpu.HBM)
     here = pl.BlockSpec(memory_space=pltpu.VMEM)
     mesh_out, grid_out, d_grid, edge_up, mesh_up, grid_up, second, w_grid, w_mesh, w_edge, vecs = pl.pallas_call(
         spread_kernel,
@@ -503,7 +536,7 @@
         scratch_shapes=[pltpu.VMEM((512, 512), BF16), pltpu.VMEM((512, 512), BF16), pltpu.VMEM((474, 512), F32),
                         pltpu.VMEM((NCHUNK, 512, 512), BF16), pltpu.VMEM((NCHUNK, 512, 512), F32),
                         pltpu.SemaphoreType.DMA((NCHUNK + 3,)), pltpu.SemaphoreType.DMA((NCHUNK + 3,))],
-        compiler_params=pltpu.CompilerParams(vmem_limit_bytes=48 * 2**20),
+        compiler_params=pltpu.CompilerParams(vmem_limit_bytes=67043328),
     )(*parts)
     return mesh_out, grid_out, d_grid, w_grid, w_mesh, w_edge, edge_up, mesh_up, grid_up, second, vecs
 
@@ -517,7 +550,7 @@
 
     def local_step(grid_in, mesh_static, edge_static, send_rows, edge_src, edge_dst, *rest):
         parts = fused_step(grid_in.T, mesh_static.T, edge_static.T, send_rows.T,
-                           edge_src.reshape(1, -1), edge_dst.reshape(1, -1), *rest)
+                           edge_src, edge_dst, *rest)
         mesh_out, grid_out, d_grid_t, *sums = spread_out(*parts)
         return (mesh_out, grid_out, d_grid_t.T) + tuple(sums)
 

time: 130 us -> 111 us (0.85)
  Pallas kernels: 123 us -> 110 us
  local copies, waits for them, and re-layouts: 5.81 us -> 0 us
    pallas_call x1, Pallas kernels: 115 us -> 101 us  [fused_step(): pl.pallas_call(step_kernel, out_shape=[jax.ShapeDtypeStruct((512, 512), B...]
    unnamed x6 -> x0, local copies, waits for them, and re-layouts: 3.28 us -> none
    reshape x2 -> x0, local copies, waits for them, and re-layouts: 2.53 us -> none  [the longest x1 1.27 us: local_step(): edge_src.reshape(1, -1)]
where the time goes in v3:
time: 111 us
  Pallas kernels  110 us (99%)
    pallas_call x1, Pallas kernels, fused_step(): pl.pallas_call(step_kernel, out_shape=[jax.ShapeDtypeStruct((512, 512), B...  101 us
    pallas_call x1, Pallas kernels, spread_out(): pl.pallas_call(spread_kernel, out_shape=[out(BF16, 512, 512), out(BF16, 5...  8.85 us

profile of v3, /device:TPU:1, one launch (start us, length us, event | category | flops | bytes accessed | tf_op | source)
XLA Modules:
  0.0 110.7 jit_solution(2178660204823263838)
XLA Ops:
  0.7 101.2 %shard_map.239 = (bf16[512,512]{1,0:T(8,128)(2,1)}, bf16[512,512]{1,0:T(8,128)(2,1)}, f32[474,512]{1,0:T(8,128)}, bf16[13,512,512]{2,1,0:T(8,128)(2,1)}) custom-call(bf16[474,512]{1,0:T(8,128)(2,1)} %bitcast.5, bf16[3,512]{1,0:T(4,128)(2,1)} %bitcast.8, bf16[4,768]{1,0:T(4,128)(2,1)} %bitcast.7, s32[16,32]{1,0:T(8,128)} %bitcast.6, s32[768]{0:T(1024)} %src_row.1, ...), custom_call_target="tpu_custom_call" | custom-call | tf_op jit(solution)/shard_map/pallas_call | solution.py:469
  101.9 8.9 %shard_map.240 = (bf16[512,512]{1,0:T(8,128)(2,1)}, bf16[512,512]{1,0:T(8,128)(2,1)}, f32[474,512]{1,0:T(8,128)}, f32[1536,512]{1,0:T(8,128)}, f32[1024,512]{1,0...) custom-call(bf16[512,512]{1,0:T(8,128)(2,1)} %get-tuple-element.26.m, ...), custom_call_target="tpu_custom_call" | custom-call | tf_op jit(solution)/shard_map/pallas_call | solution.py:529

commit v4 on v3

--- a/solution.py
+++ b/solution.py
@@ -29,103 +29,79 @@
 class Place:
     def __init__(self):
         self.p = lax.axis_index(AXIS_NAME)
-        self.c = self.p % 2
-        self.x = (self.p // 2) % 2
-        self.y = (self.p // 4) % 2
-        self.z = self.p // 8
-        self.core_peer = self.p + 1 - 2 * self.c
-        self.x_peer = self.p + 2 - 4 * self.x
-        self.y_peer = self.p + 4 - 8 * self.y
-
-    def z_peer(self, j):
-        return self.p % 8 + ((self.z + 1 + j) % 4) * 8
+        self.bit = {axis: (self.p // 2 ** i) % 2 for i, axis in enumerate('cxyuv')}
+        self.peer = {axis: self.p + 2 ** i * (1 - 2 * self.bit[axis]) for i, axis in enumerate('cxyuv')}
 
 
 class Reducer:
-    def __init__(self, at, grads, out, r0, r1, r2, r3, send, recv):
-        self.at = at
-        self.grads, self.out = grads, out
-        self.r0, self.r1, self.r2, self.r3 = r0, r1, r2, r3
-        self.send, self.recv = send, recv
-
-    def spot(self, k):
-        at = self.at
-        odd = k % 2
-        d1 = at.x * (1 - odd) + at.y * odd
-        d2 = at.y * (1 - odd) + at.x * odd
-        p1 = at.x_peer * (1 - odd) + at.y_peer * odd
-        p2 = at.y_peer * (1 - odd) + at.x_peer * odd
-        return d1, d2, p1, p2
-
-    def copies(self, s, k):
-        at = self.at
-        d1, d2, p1, p2 = self.spot(k)
-
-        def make(src, dst, lane, dev):
-            return pltpu.make_async_remote_copy(
-                src_ref=src, dst_ref=dst, send_sem=self.send.at[k, lane], recv_sem=self.recv.at[k, lane],
-                device_id=(dev,), device_id_type=pl.DeviceIdType.MESH)
-
-        def rows(start, size):
-            return pl.ds(pl.multiple_of(start, 64), size)
-
-        row1 = at.c * 256 + d1 * 128
-        row2 = row1 + d2 * 64
-        if s == 0:
-            return [make(self.grads.at[k, rows((1 - at.c) * 256, 256)], self.r0.at[k], 0, at.core_peer)]
-        if s == 1:
-            return [make(self.grads.at[k, rows(at.c * 256 + (1 - d1) * 128, 128)], self.r1.at[k], 1, p1)]
-        if s == 2:
-            return [make(self.grads.at[k, rows(row1 + (1 - d2) * 64, 64)], self.r2.at[k], 2, p2)]
-        if s == 3:
-            cols = [pl.ds(pl.multiple_of(((at.z + 1 + j) % 4) * 128, 128), 128) for j in range(3)]
-            return [make(self.grads.at[k, rows(row2, 64), cols[j]], self.r3.at[k, j], 3 + j, at.z_peer(j)) for j in range(3)]
-        if s == 4:
-            part = self.out.at[k, rows(row2, 64), pl.ds(pl.multiple_of(at.z * 128, 128), 128)]
-            return [make(part, part, 6 + j, at.z_peer(j)) for j in range(3)]
-        if s == 5:
-            part = self.out.at[k, rows(row2, 64)]
-            return [make(part, part, 9, p2)]
-        if s == 6:
-            part = self.out.at[k, rows(row1, 128)]
-            return [make(part, part, 10, p1)]
-        part = self.out.at[k, rows(at.c * 256, 256)]
-        return [make(part, part, 11, at.core_peer)]
+    def __init__(self, at, grads, land, out, send, recv):
+        self.at, self.grads, self.land, self.out, self.send, self.recv = at, grads, land, out, send, recv
+
+    def axes(self, k):
+        return 'c' + AXES[k]
+
+    def regions(self, k):
+        row, rows, col, cols = 0, 512, 0, 512
+        kept, sent = [], []
+        for axis in self.axes(k):
+            bit = self.at.bit[axis]
+            if axis in 'cxy':
+                rows //= 2
+                sent.append((row + (1 - bit) * rows, rows, col, cols))
+                row = row + bit * rows
+            else:
+                cols //= 2
+                sent.append((row, rows, col + (1 - bit) * cols, cols))
+                col = col + bit * cols
+            kept.append((row, rows, col, cols))
+        return kept, sent
+
+    def index(self, k, region, step=0, tile=None):
+        row, rows, col, cols = region
+        lanes = pl.ds(0, 512) if cols == 512 else pl.ds(pl.multiple_of(col, 128), cols)
+        return k, pl.ds(pl.multiple_of(row + step, 64), tile or rows), lanes
+
+    def copy(self, s, k):
+        kept, sent = self.regions(k)
+        turn = s if s < 5 else 9 - s
+        if s < 5:
+            src, dst = self.grads.at[self.index(k, sent[s])], self.land.at[self.index(k, kept[s])]
+        else:
+            src = dst = self.out.at[self.index(k, kept[turn])]
+        return pltpu.make_async_remote_copy(
+            src_ref=src, dst_ref=dst, send_sem=self.send.at[k, s], recv_sem=self.recv.at[k, s],
+            device_id=(self.at.peer[self.axes(k)[turn]],), device_id_type=pl.DeviceIdType.MESH)
 
     def start(self, s, k):
-        for copy in self.copies(s, k):
-            copy.start()
+        self.copy(s, k).start()
 
     def stage(self, s, k):
-        at = self.at
-        d1, d2, _, _ = self.spot(k)
-        for copy in self.copies(s, k):
-            copy.wait_recv()
-        row1 = at.c * 256 + d1 * 128
-        row2 = row1 + d2 * 64
-        if s < 3:
-            start, size, landed = ((at.c * 256, 256, self.r0), (row1, 128, self.r1), (row2, 64, self.r2))[s]
-
-            @pl.loop(0, size // 64)
-            def _(i):
-                mine = (k, pl.ds(pl.multiple_of(start + i * 64, 64), 64))
-                theirs = landed[k, pl.ds(pl.multiple_of(i * 64, 64), 64)]
-                self.grads[mine] = (self.grads[mine].astype(F32) + theirs.astype(F32)).astype(BF16)
-        elif s == 3:
-            spot = (k, pl.ds(pl.multiple_of(row2, 64), 64), pl.ds(pl.multiple_of(at.z * 128, 128), 128))
-            total = self.grads[spot].astype(F32)
-            for j in range(3):
-                total = total + self.r3[k, j].astype(F32)
-            self.out[spot] = total.astype(BF16)
-        if s < 7:
+        self.copy(s, k).wait_recv()
+        if s < 5:
+            kept, sent = self.regions(k)
+            into = self.out if s == 4 else self.grads
+
+            def add(step):
+                mine = self.index(k, kept[s], step, 64)
+                theirs = self.land[self.index(k, sent[s], step, 64)]
+                into[mine] = (self.grads[mine].astype(F32) + theirs.astype(F32)).astype(BF16)
+
+            if kept[s][1] == 64:
+                add(0)
+            else:
+                @pl.loop(0, kept[s][1] // 64)
+                def _(i):
+                    add(i * 64)
+        if s < 9:
             self.start(s + 1, k)
 
-    def drain(self, k):
-        for s in range(8):
-            for copy in self.copies(s, k):
-                copy.wait_send()
-
-
+    def drain(self):
+        for k in range(NCHUNK):
+            for s in range(10):
+                self.copy(s, k).wait_send()
+
+
+AXES = ('xvuy', 'yuvx', 'uyxv', 'yxuv', 'xyuv', 'yxuv', 'xyuv', 'uvxy', 'xyuv', 'yxuv', 'xyuv', 'yxuv', 'xyuv')
 ORDER = (
         (),
         (),
@@ -133,26 +109,27 @@
         (),
         (0, 1),
         (16, 17),
-        (32,),
-        (),
-        (),
-        (),
-        (),
-        (),
-        (),
-        (),
-        (33,),
-        (2,),
-        (48, 3),
-        (4, 5),
-        (19, 6, 18),
-        (8, 20),
-        (49, 34, 7, 21),
-        (64, 35),
-        (22, 9, 65, 36, 10),
-        (37, 23, 80, 50, 24, 81, 12, 38, 51, 11, 25, 52, 26, 39, 53, 97, 40, 66, 96, 68, 67, 54, 27, 55, 41, 42, 112,
-     69, 28, 113, 82, 70, 83, 56, 43, 44, 85, 84, 57, 71, 98, 58, 100, 86, 72, 59, 87, 99, 114, 60, 101, 73, 74, 88,
-     116, 115, 102, 75, 89, 76, 90, 117, 103, 104, 91, 105, 92, 119, 106, 121, 120, 107, 118, 108, 122, 123, 124),
+        (),
+        (32, 33),
+        (48,),
+        (),
+        (),
+        (),
+        (),
+        (),
+        (64,),
+        (),
+        (49,),
+        (4, 2, 3, 5, 65, 80),
+        (6,),
+        (81, 7, 19, 20, 8, 96, 18),
+        (22,),
+        (97, 21, 9, 36, 34, 23),
+        (10,),
+        (35, 24, 38, 52, 12, 113, 37, 50, 51, 54, 112, 68, 40, 53, 26, 66, 11, 67, 28, 39, 129, 70, 84, 69, 42, 56, 25,
+     83, 86, 82, 100, 55, 27, 85, 72, 99, 41, 128, 58, 98, 44, 101, 71, 145, 43, 116, 102, 57, 88, 60, 144, 115, 74, 59,
+     114, 118, 73, 87, 104, 76, 132, 90, 117, 120, 131, 75, 89, 92, 134, 130, 106, 103, 147, 105, 136, 122, 91, 108,
+     121, 119, 133, 107, 124, 150, 138, 123, 146, 137, 135, 140, 153, 139, 156, 149, 148, 151, 154, 152, 155),
 )
 
 
@@ -166,7 +143,7 @@
     def poll(self):
         for code in ORDER[self.point]:
             self.red.stage(code // 16, code % 16)
-            if code // 16 == 7:
+            if code // 16 == 9:
                 self.stores[code % 16].start()
         self.point += 1
 
@@ -180,7 +157,7 @@
                 mesh_out_h, grid_out_h, d_grid_h, sums_h,
                 grid_t, w_grid_in, w_edge_up, w_mesh_up, w_grid_up, w_second, d_mesh_out, d_grid_out,
                 mesh_out, grid_out, d_grid_t, sums, load_sem, store_sem,
-                grads, r0, r1, r2, r3, red_send, red_recv, a2a_send, a2a_recv,
+                grads, land, red_send, red_recv, a2a_send, a2a_recv,
                 hid0, dsl0, nrm0, inv0, hid1, dsl1, nrm1, inv1, hid2, dsl2, nrm2, inv2, hid3, dsl3, nrm3, inv3,
                 hid_s, dlin_s, dpre_s, dlin3, dpre3, dpre4,
                 pick_send, pick_src, pick_dst, grid_lat, mesh_lat, cat, edge_new, agg, d_agg, d_edge,
@@ -208,7 +185,7 @@
     def _(r):
         pl.semaphore_signal(barrier, inc=1, device_id=((at.p + r) % n_dev,), device_id_type=pl.DeviceIdType.MESH)
 
-    red = Reducer(at, grads, sums, r0, r1, r2, r3, red_send, red_recv)
+    red = Reducer(at, grads, land, sums, red_send, red_recv)
     prog = Progress(red, stores)
 
     def vec(k, j):
@@ -357,7 +334,9 @@
     def _(i, rows):
         out = tail_saved(2, contract_rows(edge_t[:, rows], w_edge_in[...]), rows, saves2)
         cat[rows, pl.ds(0, 512)] = out.astype(BF16)
-        cat[rows, pl.ds(1024, 512)] = contract_rows(pick_dst[:, rows], mesh_lat[...]).astype(BF16)
+        recv = contract_rows(pick_dst[:, rows], mesh_lat[...]).astype(BF16)
+        cat[rows, pl.ds(1024, 512)] = recv
+        nrm3[rows, :] = matmul(out.astype(BF16), w_edge_up[pl.ds(0, 512), :]) + matmul(recv, w_edge_up[pl.ds(1024, 512), :])
 
     prog.poll()
     exchange(outgoing, incoming, 0, False)
@@ -365,8 +344,9 @@
     @pl.loop(0, 3)
     def _(i):
         rows = rows_of(i)
-        cat[rows, pl.ds(512, 512)] = contract_rows(pick_src[:, rows], incoming[...]).astype(BF16)
-        upd = tail_saved(3, matmul(cat[rows, :], w_edge_up[...]), rows, saves3)
+        sender = contract_rows(pick_src[:, rows], incoming[...]).astype(BF16)
+        cat[rows, pl.ds(512, 512)] = sender
+        upd = tail_saved(3, nrm3[rows, :] + matmul(sender, w_edge_up[pl.ds(512, 512), :]), rows, saves3)
         edge_new[rows, :] = (cat[rows, pl.ds(0, 512)].astype(F32) + upd).astype(BF16)
 
     @tiles(2)
@@ -435,9 +415,7 @@
     prog.ready(11)
     prog.poll()
 
-    @pl.loop(0, NCHUNK)
-    def _(k):
-        red.drain(k)
+    red.drain()
 
     for copy in stores:
         copy.wait()
@@ -457,8 +435,7 @@
         bf16(474, 512), bf16(474, 512), bf16(1536, 512), bf16(1024, 512), bf16(512, 512), bf16(6, 512, 512), bf16(512, 512),
         bf16(512, 512), bf16(512, 512), bf16(512, 512), f32(474, 512), bf16(NCHUNK, 512, 512),
         pltpu.SemaphoreType.DMA((13,)), pltpu.SemaphoreType.DMA((NCHUNK + 3,)),
-        bf16(NCHUNK, 512, 512), bf16(NCHUNK, 256, 512), bf16(NCHUNK, 128, 512), bf16(NCHUNK, 64, 512), bf16(NCHUNK, 3, 64, 128),
-        pltpu.SemaphoreType.DMA((NCHUNK, 12)), pltpu.SemaphoreType.DMA((NCHUNK, 12)),
+        bf16(NCHUNK, 512, 512), bf16(NCHUNK, 512, 512), pltpu.SemaphoreType.DMA((NCHUNK, 10)), pltpu.SemaphoreType.DMA((NCHUNK, 10)),
         pltpu.SemaphoreType.DMA((2, 32)), pltpu.SemaphoreType.DMA((2, 32)),
         *saves(512), *saves(512), *saves(768), *saves(768),
         bf16(768, 512), bf16(768, 512), bf16(768, 512), bf16(768, 512), bf16(768, 512), bf16(512, 512),

time: 111 us -> 113 us (1.018)
  Pallas kernels: 110 us -> 112 us
    pallas_call x1, Pallas kernels: 101 us -> 103 us  [fused_step(): pl.pallas_call(step_kernel, out_shape=[jax.ShapeDtypeStruct((512, 512), B...]
where the time goes in v4:
time: 113 us
  Pallas kernels  112 us (99%)
    pallas_call x1, Pallas kernels, fused_step(): pl.pallas_call(step_kernel, out_shape=[jax.ShapeDtypeStruct((512, 512), B...  103 us
    pallas_call x1, Pallas kernels, spread_out(): pl.pallas_call(spread_kernel, out_shape=[out(BF16, 512, 512), out(BF16, 5...  8.85 us

profile of v4, /device:TPU:1, one launch (start us, length us, event | category | flops | bytes accessed | tf_op | source)
XLA Modules:
  0.0 113.0 jit_solution(14959550301196344238)
XLA Ops:
  0.7 103.5 %shard_map.239 = (bf16[512,512]{1,0:T(8,128)(2,1)}, bf16[512,512]{1,0:T(8,128)(2,1)}, f32[474,512]{1,0:T(8,128)}, bf16[13,512,512]{2,1,0:T(8,128)(2,1)}) custom-call(bf16[474,512]{1,0:T(8,128)(2,1)} %bitcast.5, bf16[3,512]{1,0:T(4,128)(2,1)} %bitcast.8, bf16[4,768]{1,0:T(4,128)(2,1)} %bitcast.7, s32[16,32]{1,0:T(8,128)} %bitcast.6, s32[768]{0:T(1024)} %src_row.1, ...), custom_call_target="tpu_custom_call" | custom-call | tf_op jit(solution)/shard_map/pallas_call | solution.py:446
  104.1 8.9 %shard_map.240 = (bf16[512,512]{1,0:T(8,128)(2,1)}, bf16[512,512]{1,0:T(8,128)(2,1)}, f32[474,512]{1,0:T(8,128)}, f32[1536,512]{1,0:T(8,128)}, f32[1024,512]{1,0...) custom-call(bf16[512,512]{1,0:T(8,128)(2,1)} %get-tuple-element.26.m, ...), custom_call_target="tpu_custom_call" | custom-call | tf_op jit(solution)/shard_map/pallas_call | solution.py:506

commit v5 on v3

--- a/solution.py
+++ b/solution.py
@@ -138,21 +138,21 @@
         (),
         (),
         (),
-        (),
-        (),
-        (),
         (33,),
+        (48,),
+        (),
+        (),
         (2,),
-        (48, 3),
+        (3,),
         (4, 5),
-        (19, 6, 18),
-        (8, 20),
-        (49, 34, 7, 21),
-        (64, 35),
-        (22, 9, 65, 36, 10),
-        (37, 23, 80, 50, 24, 81, 12, 38, 51, 11, 25, 52, 26, 39, 53, 97, 40, 66, 96, 68, 67, 54, 27, 55, 41, 42, 112,
-     69, 28, 113, 82, 70, 83, 56, 43, 44, 85, 84, 57, 71, 98, 58, 100, 86, 72, 59, 87, 99, 114, 60, 101, 73, 74, 88,
-     116, 115, 102, 75, 89, 76, 90, 117, 103, 104, 91, 105, 92, 119, 106, 121, 120, 107, 118, 108, 122, 123, 124),
+        (18, 6),
+        (7, 21),
+        (20, 19, 34, 8, 49),
+        (64, 37, 22, 35),
+        (23,),
+        (36, 65, 9, 10, 80, 53, 24, 38, 11, 52, 51, 50, 26, 40, 25, 39, 81, 54, 12, 69, 67, 68, 42, 56, 66, 27, 41, 28,
+     84, 83, 70, 55, 82, 44, 43, 97, 96, 85, 113, 72, 57, 71, 99, 86, 58, 100, 87, 98, 59, 73, 60, 101, 88, 74, 89, 75,
+     102, 103, 90, 76, 104, 91, 105, 116, 118, 92, 115, 106, 120, 107, 121, 117, 108, 122, 112, 123, 119, 114, 124),
 )
 
 
@@ -260,24 +260,27 @@
             grads[k, rows_of(i), :] = part.astype(BF16)
 
     def exchange(src, dst, lane, start):
-        def copy(r):
-            to = (at.p + r) % n_dev
+        low = at.p % 8
+
+        def copy(turn, j):
+            peer_z = (at.z % 2 + turn % 2) % 2 + 2 * ((at.z // 2 + turn // 2) % 2)
+            to = peer_z * 8 + (low + j) % 8
             return pltpu.make_async_remote_copy(
                 src_ref=src.at[pl.ds(pl.multiple_of(to * 16, 16), 16)], dst_ref=dst.at[pl.ds(pl.multiple_of(at.p * 16, 16), 16)],
-                send_sem=a2a_send.at[lane, r], recv_sem=a2a_recv.at[lane, r],
+                send_sem=a2a_send.at[lane, turn * 8 + j], recv_sem=a2a_recv.at[lane, turn * 8 + j],
                 device_id=(to,), device_id_type=pl.DeviceIdType.MESH)
 
+        for turn in (3, 2, 1, 0):
+            @pl.loop(0 if turn else 1, 8)
+            def _(j):
+                if start:
+                    copy(turn, j).start()
+                else:
+                    copy(turn, j).wait()
+
         if start:
-            @pl.loop(1, n_dev)
-            def _(r):
-                copy(r).start()
-
             mine = pl.ds(pl.multiple_of(at.p * 16, 16), 16)
             dst[mine, :] = src[mine, :]
-        else:
-            @pl.loop(1, n_dev)
-            def _(r):
-                copy(r).wait()
 
     saves0 = (hid0, dsl0, nrm0, inv0)
     saves1 = (hid1, dsl1, nrm1, inv1)
@@ -357,7 +360,9 @@
     def _(i, rows):
         out = tail_saved(2, contract_rows(edge_t[:, rows], w_edge_in[...]), rows, saves2)
         cat[rows, pl.ds(0, 512)] = out.astype(BF16)
-        cat[rows, pl.ds(1024, 512)] = contract_rows(pick_dst[:, rows], mesh_lat[...]).astype(BF16)
+        recv = contract_rows(pick_dst[:, rows], mesh_lat[...]).astype(BF16)
+        cat[rows, pl.ds(1024, 512)] = recv
+        nrm3[rows, :] = matmul(out.astype(BF16), w_edge_up[pl.ds(0, 512), :]) + matmul(recv, w_edge_up[pl.ds(1024, 512), :])
 
     prog.poll()
     exchange(outgoing, incoming, 0, False)
@@ -365,8 +370,9 @@
     @pl.loop(0, 3)
     def _(i):
         rows = rows_of(i)
-        cat[rows, pl.ds(512, 512)] = contract_rows(pick_src[:, rows], incoming[...]).astype(BF16)
-        upd = tail_saved(3, matmul(cat[rows, :], w_edge_up[...]), rows, saves3)
+        sender = contract_rows(pick_src[:, rows], incoming[...]).astype(BF16)
+        cat[rows, pl.ds(512, 512)] = sender
+        upd = tail_saved(3, nrm3[rows, :] + matmul(sender, w_edge_up[pl.ds(512, 512), :]), rows, saves3)
         edge_new[rows, :] = (cat[rows, pl.ds(0, 512)].astype(F32) + upd).astype(BF16)
 
     @tiles(2)

time: 111 us -> 112 us (level)
  no operation moved by 1% of the time
where the time goes in v5:
time: 112 us; the launch traced here: 111 us
  Pallas kernels  111 us (99%)
    pallas_call x1, Pallas kernels, fused_step(): pl.pallas_call(step_kernel, out_shape=[jax.ShapeDtypeStruct((512, 512), B...  102 us
    pallas_call x1, Pallas kernels, spread_out(): pl.pallas_call(spread_kernel, out_shape=[out(BF16, 512, 512), out(BF16, 5...  8.85 us

profile of v5, /device:TPU:1, one launch (start us, length us, event | category | flops | bytes accessed | tf_op | source)
XLA Modules:
  0.0 111.4 jit_solution(17068339434785863927)
XLA Ops:
  0.7 101.9 %shard_map.239 = (bf16[512,512]{1,0:T(8,128)(2,1)}, bf16[512,512]{1,0:T(8,128)(2,1)}, f32[474,512]{1,0:T(8,128)}, bf16[13,512,512]{2,1,0:T(8,128)(2,1)}) custom-call(bf16[474,512]{1,0:T(8,128)(2,1)} %bitcast.5, bf16[3,512]{1,0:T(4,128)(2,1)} %bitcast.8, bf16[4,768]{1,0:T(4,128)(2,1)} %bitcast.7, s32[16,32]{1,0:T(8,128)} %bitcast.6, s32[768]{0:T(1024)} %src_row.1, ...), custom_call_target="tpu_custom_call" | custom-call | tf_op jit(solution)/shard_map/pallas_call | solution.py:475
  102.6 8.9 %shard_map.240 = (bf16[512,512]{1,0:T(8,128)(2,1)}, bf16[512,512]{1,0:T(8,128)(2,1)}, f32[474,512]{1,0:T(8,128)}, f32[1536,512]{1,0:T(8,128)}, f32[1024,512]{1,0...) custom-call(bf16[512,512]{1,0:T(8,128)(2,1)} %get-tuple-element.26.m, ...), custom_call_target="tpu_custom_call" | custom-call | tf_op jit(solution)/shard_map/pallas_call | solution.py:535

commit v6 on v3

--- a/solution.py
+++ b/solution.py
@@ -260,24 +260,27 @@
             grads[k, rows_of(i), :] = part.astype(BF16)
 
     def exchange(src, dst, lane, start):
-        def copy(r):
-            to = (at.p + r) % n_dev
+        low = at.p % 8
+
+        def copy(turn, j):
+            peer_z = (at.z % 2 + turn % 2) % 2 + 2 * ((at.z // 2 + turn // 2) % 2)
+            to = peer_z * 8 + (low + j) % 8
             return pltpu.make_async_remote_copy(
                 src_ref=src.at[pl.ds(pl.multiple_of(to * 16, 16), 16)], dst_ref=dst.at[pl.ds(pl.multiple_of(at.p * 16, 16), 16)],
-                send_sem=a2a_send.at[lane, r], recv_sem=a2a_recv.at[lane, r],
+                send_sem=a2a_send.at[lane, turn * 8 + j], recv_sem=a2a_recv.at[lane, turn * 8 + j],
                 device_id=(to,), device_id_type=pl.DeviceIdType.MESH)
 
+        for turn in (3, 2, 1, 0):
+            @pl.loop(0 if turn else 1, 8)
+            def _(j):
+                if start:
+                    copy(turn, j).start()
+                else:
+                    copy(turn, j).wait()
+
         if start:
-            @pl.loop(1, n_dev)
-            def _(r):
-                copy(r).start()
-
             mine = pl.ds(pl.multiple_of(at.p * 16, 16), 16)
             dst[mine, :] = src[mine, :]
-        else:
-            @pl.loop(1, n_dev)
-            def _(r):
-                copy(r).wait()
 
     saves0 = (hid0, dsl0, nrm0, inv0)
     saves1 = (hid1, dsl1, nrm1, inv1)
@@ -482,7 +485,8 @@
 
 
 def spread_kernel(mesh_in, grid_in, d_grid_in, sums, mesh_out, grid_out, d_grid_out, edge_up, mesh_up, grid_up, second,
-                  w_grid, w_mesh, w_edge, vecs, mesh_buf, grid_buf, d_grid_buf, sum_buf, wide, sem_in, sem_out):
+                  w_grid_h, w_mesh_h, w_edge_h, vecs_h, mesh_buf, grid_buf, d_grid_buf, sum_buf, wide, w_grid, w_mesh, w_edge, vecs,
+                  sem_in, sem_out):
     loads = [pltpu.make_async_copy(sums.at[k], sum_buf.at[k], sem_in.at[k]) for k in range(NCHUNK)]
     through = [(mesh_in, mesh_buf, mesh_out), (grid_in, grid_buf, grid_out), (d_grid_in, d_grid_buf, d_grid_out)]
     heads = [pltpu.make_async_copy(a, b, sem_in.at[NCHUNK + i]) for i, (a, b, _) in enumerate(through)]
@@ -502,6 +506,9 @@
     w_edge[...] = misc[477:481]
     for k in range(6):
         vecs[k] = misc[481 + 4 * k:485 + 4 * k]
+    for i, (buf, out) in enumerate([(w_grid, w_grid_h), (w_mesh, w_mesh_h), (w_edge, w_edge_h), (vecs, vecs_h)]):
+        stores.append(pltpu.make_async_copy(buf, out, sem_out.at[NCHUNK + 3 + i]))
+        stores[-1].start()
     for k, (out, part) in HOME.items():
         loads[k].wait()
 
@@ -525,17 +532,18 @@
         return jax.ShapeDtypeStruct(shape, dtype)
 
     anywhere = pl.BlockSpec(memory_space=pltpu.HBM)
-    here = pl.BlockSpec(memory_space=pltpu.VMEM)
     mesh_out, grid_out, d_grid, edge_up, mesh_up, grid_up, second, w_grid, w_mesh, w_edge, vecs = pl.pallas_call(
         spread_kernel,
         out_shape=[out(BF16, 512, 512), out(BF16, 512, 512), out(F32, 474, 512), out(F32, 1536, 512), out(F32, 1024, 512),
                    out(F32, 512, 512), out(F32, 6, 512, 512), out(F32, 474, 512), out(F32, 3, 512), out(F32, 4, 512),
                    out(F32, 6, 4, 512)],
         in_specs=[anywhere] * 4,
-        out_specs=[anywhere] * 7 + [here] * 4,
+        out_specs=[anywhere] * 11,
         scratch_shapes=[pltpu.VMEM((512, 512), BF16), pltpu.VMEM((512, 512), BF16), pltpu.VMEM((474, 512), F32),
                         pltpu.VMEM((NCHUNK, 512, 512), BF16), pltpu.VMEM((NCHUNK, 512, 512), F32),
-                        pltpu.SemaphoreType.DMA((NCHUNK + 3,)), pltpu.SemaphoreType.DMA((NCHUNK + 3,))],
+                        pltpu.VMEM((474, 512), F32), pltpu.VMEM((3, 512), F32), pltpu.VMEM((4, 512), F32),
+                        pltpu.VMEM((6, 4, 512), F32),
+                        pltpu.SemaphoreType.DMA((NCHUNK + 3,)), pltpu.SemaphoreType.DMA((NCHUNK + 7,))],
         compiler_params=pltpu.CompilerParams(vmem_limit_bytes=67043328),
     )(*parts)
     return mesh_out, grid_out, d_grid, w_grid, w_mesh, w_edge, edge_up, mesh_up, grid_up, second, vecs

time: 111 us -> 112 us (level)
    pallas_call x1, Pallas kernels: 101 us -> 103 us  [fused_step(): pl.pallas_call(step_kernel, out_shape=[jax.ShapeDtypeStruct((512, 512), B...]
where the time goes in v6:
time: 112 us
  Pallas kernels  111 us (99%)
    pallas_call x1, Pallas kernels, fused_step(): pl.pallas_call(step_kernel, out_shape=[jax.ShapeDtypeStruct((512, 512), B...  103 us
    pallas_call x1, Pallas kernels, spread_out(): pl.pallas_call(spread_kernel, out_shape=[out(BF16, 512, 512), out(BF16, 5...  8.36 us

profile of v6, /device:TPU:1, one launch (start us, length us, event | category | flops | bytes accessed | tf_op | source)
XLA Modules:
  0.0 111.7 jit_solution(11252887840809116943)
XLA Ops:
  0.7 102.7 %shard_map.239 = (bf16[512,512]{1,0:T(8,128)(2,1)}, bf16[512,512]{1,0:T(8,128)(2,1)}, f32[474,512]{1,0:T(8,128)}, bf16[13,512,512]{2,1,0:T(8,128)(2,1)}) custom-call(bf16[474,512]{1,0:T(8,128)(2,1)} %bitcast.5, bf16[3,512]{1,0:T(4,128)(2,1)} %bitcast.8, bf16[4,768]{1,0:T(4,128)(2,1)} %bitcast.7, s32[16,32]{1,0:T(8,128)} %bitcast.6, s32[768]{0:T(1024)} %src_row.1, ...), custom_call_target="tpu_custom_call" | custom-call | tf_op jit(solution)/shard_map/pallas_call | solution.py:472
  103.4 8.4 %shard_map.240 = (bf16[512,512]{1,0:T(8,128)(2,1)}, bf16[512,512]{1,0:T(8,128)(2,1)}, f32[474,512]{1,0:T(8,128)}, f32[1536,512]{1,0:T(8,128)}, f32[1024,512]{1,0...) custom-call(bf16[512,512]{1,0:T(8,128)(2,1)} %get-tuple-element.26.m, ...), custom_call_target="tpu_custom_call" | custom-call | tf_op jit(solution)/shard_map/pallas_call | solution.py:535

commit v7 on v3

--- a/solution.py
+++ b/solution.py
@@ -482,7 +482,8 @@
 
 
 def spread_kernel(mesh_in, grid_in, d_grid_in, sums, mesh_out, grid_out, d_grid_out, edge_up, mesh_up, grid_up, second,
-                  w_grid, w_mesh, w_edge, vecs, mesh_buf, grid_buf, d_grid_buf, sum_buf, wide, sem_in, sem_out):
+                  w_grid_h, w_mesh_h, w_edge_h, vecs_h, mesh_buf, grid_buf, d_grid_buf, sum_buf, wide, w_grid, w_mesh, w_edge, vecs,
+                  sem_in, sem_out):
     loads = [pltpu.make_async_copy(sums.at[k], sum_buf.at[k], sem_in.at[k]) for k in range(NCHUNK)]
     through = [(mesh_in, mesh_buf, mesh_out), (grid_in, grid_buf, grid_out), (d_grid_in, d_grid_buf, d_grid_out)]
     heads = [pltpu.make_async_copy(a, b, sem_in.at[NCHUNK + i]) for i, (a, b, _) in enumerate(through)]
@@ -502,6 +503,9 @@
     w_edge[...] = misc[477:481]
     for k in range(6):
         vecs[k] = misc[481 + 4 * k:485 + 4 * k]
+    for i, (buf, out) in enumerate([(w_grid, w_grid_h), (w_mesh, w_mesh_h), (w_edge, w_edge_h), (vecs, vecs_h)]):
+        stores.append(pltpu.make_async_copy(buf, out, sem_out.at[NCHUNK + 3 + i]))
+        stores[-1].start()
     for k, (out, part) in HOME.items():
         loads[k].wait()
 
@@ -525,17 +529,18 @@
         return jax.ShapeDtypeStruct(shape, dtype)
 
     anywhere = pl.BlockSpec(memory_space=pltpu.HBM)
-    here = pl.BlockSpec(memory_space=pltpu.VMEM)
     mesh_out, grid_out, d_grid, edge_up, mesh_up, grid_up, second, w_grid, w_mesh, w_edge, vecs = pl.pallas_call(
         spread_kernel,
         out_shape=[out(BF16, 512, 512), out(BF16, 512, 512), out(F32, 474, 512), out(F32, 1536, 512), out(F32, 1024, 512),
                    out(F32, 512, 512), out(F32, 6, 512, 512), out(F32, 474, 512), out(F32, 3, 512), out(F32, 4, 512),
                    out(F32, 6, 4, 512)],
         in_specs=[anywhere] * 4,
-        out_specs=[anywhere] * 7 + [here] * 4,
+        out_specs=[anywhere] * 11,
         scratch_shapes=[pltpu.VMEM((512, 512), BF16), pltpu.VMEM((512, 512), BF16), pltpu.VMEM((474, 512), F32),
                         pltpu.VMEM((NCHUNK, 512, 512), BF16), pltpu.VMEM((NCHUNK, 512, 512), F32),
-                        pltpu.SemaphoreType.DMA((NCHUNK + 3,)), pltpu.SemaphoreType.DMA((NCHUNK + 3,))],
+                        pltpu.VMEM((474, 512), F32), pltpu.VMEM((3, 512), F32), pltpu.VMEM((4, 512), F32),
+                        pltpu.VMEM((6, 4, 512), F32),
+                        pltpu.SemaphoreType.DMA((NCHUNK + 3,)), pltpu.SemaphoreType.DMA((NCHUNK + 7,))],
         compiler_params=pltpu.CompilerParams(vmem_limit_bytes=67043328),
     )(*parts)
     return mesh_out, grid_out, d_grid, w_grid, w_mesh, w_edge, edge_up, mesh_up, grid_up, second, vecs

time: 111 us -> 110 us (level)
  no operation moved by 1% of the time
where the time goes in v7:
time: 110 us
  Pallas kernels  110 us (100%)
    pallas_call x1, Pallas kernels, fused_step(): pl.pallas_call(step_kernel, out_shape=[jax.ShapeDtypeStruct((512, 512), B...  101 us
    pallas_call x1, Pallas kernels, spread_out(): pl.pallas_call(spread_kernel, out_shape=[out(BF16, 512, 512), out(BF16, 5...  8.36 us

profile of v7, /device:TPU:1, one launch (start us, length us, event | category | flops | bytes accessed | tf_op | source)
XLA Modules:
  0.0 110.2 jit_solution(2139611651497188307)
XLA Ops:
  0.7 101.2 %shard_map.239 = (bf16[512,512]{1,0:T(8,128)(2,1)}, bf16[512,512]{1,0:T(8,128)(2,1)}, f32[474,512]{1,0:T(8,128)}, bf16[13,512,512]{2,1,0:T(8,128)(2,1)}) custom-call(bf16[474,512]{1,0:T(8,128)(2,1)} %bitcast.5, bf16[3,512]{1,0:T(4,128)(2,1)} %bitcast.8, bf16[4,768]{1,0:T(4,128)(2,1)} %bitcast.7, s32[16,32]{1,0:T(8,128)} %bitcast.6, s32[768]{0:T(1024)} %src_row.1, ...), custom_call_target="tpu_custom_call" | custom-call | tf_op jit(solution)/shard_map/pallas_call | solution.py:469
  101.9 8.4 %shard_map.240 = (bf16[512,512]{1,0:T(8,128)(2,1)}, bf16[512,512]{1,0:T(8,128)(2,1)}, f32[474,512]{1,0:T(8,128)}, f32[1536,512]{1,0:T(8,128)}, f32[1024,512]{1,0...) custom-call(bf16[512,512]{1,0:T(8,128)(2,1)} %get-tuple-element.26.m, ...), custom_call_target="tpu_custom_call" | custom-call | tf_op jit(solution)/shard_map/pallas_call | solution.py:532
